TPU v7x, 32 devices: a whole 2x2x4 slice. The times are simulated.
32 devices in a mesh: fsdp: 4 (over y, x), expert: 8 (over z, core).
Axes of the slice: x: 2, y: 2, z: 4, core: 2. Of those that a mesh axis runs over, the one named last changes fastest.
Arguments:
- tokens: bfloat16 [8192, 2048], P(('fsdp', 'expert')), may hold values from -6 to 6
- segments: int32 [32, 256], P(('fsdp', 'expert')), may hold values from 0 to 7, never falling along the last dimension, each value on 1 to 128 neighbouring positions
- routes: int32 [8192, 8], P(('fsdp', 'expert')), may hold values from 0 to 31, all different within a row; in each aligned block of 256 rows (0 to 255, 256 to 511, ...) at most 80 rows name the same one
- attn_gain: bfloat16 [2048], P('expert'), may hold values from 0.5 to 1.5
- w_query: bfloat16 [2048, 4096], P('expert', 'fsdp'), may hold values from -0.125 to 0.125
- key_matrix: bfloat16 [2048, 512], P('expert', 'fsdp'), may hold values from -0.125 to 0.125
- value_matrix: bfloat16 [2048, 512], P('expert', 'fsdp'), may hold values from -0.125 to 0.125
- output_matrix: bfloat16 [4096, 2048], P(('fsdp', 'expert')), may hold values from -0.25 to 0.25
- query_gain: bfloat16 [128], replicated, may hold values from 0.6 to 4
- key_gain: bfloat16 [128], replicated, may hold values from 0.6 to 4
- ffn_gain: bfloat16 [2048], P('expert'), may hold values from 0.5 to 1.5
- w_router: bfloat16 [2048, 32], P('expert'), may hold values from -0.0625 to 0.0625
- w_gate: bfloat16 [32, 2048, 768], P(('fsdp', 'expert')), may hold values from -0.125 to 0.125
- w_up: bfloat16 [32, 2048, 768], P(('fsdp', 'expert')), may hold values from -0.125 to 0.125
- w_down: bfloat16 [32, 768, 2048], P(('fsdp', 'expert')), may hold values from -0.625 to 0.625
- cotangent: bfloat16 [8192, 2048], P(('fsdp', 'expert')), may hold values from -6 to 6
Outputs:
- output: bfloat16 [8192, 2048], P(('fsdp', 'expert'))
- token_grad: float32 [8192, 2048], P(('fsdp', 'expert'))
- attn_gain_grad: float32 [2048], P('expert')
- query_weight_grad: float32 [2048, 4096], P('expert', 'fsdp')
- key_weight_grad: float32 [2048, 512], P('expert', 'fsdp')
- value_weight_grad: float32 [2048, 512], P('expert', 'fsdp')
- out_weight_grad: float32 [4096, 2048], P(('fsdp', 'expert'))
- query_gain_grad: float32 [128], replicated
- key_gain_grad: float32 [128], replicated
- ffn_gain_grad: float32 [2048], P('expert')
- router_grad: float32 [2048, 32], P('expert')
- gate_grad: float32 [32, 2048, 768], P(('fsdp', 'expert'))
- up_grad: float32 [32, 2048, 768], P(('fsdp', 'expert'))
- down_grad: float32 [32, 768, 2048], P(('fsdp', 'expert'))
Inputs may be any that keep to these rules, and one draw needn't show every extreme that they name: `routes`: each token names 8 different experts. Among the 256 tokens of one device no expert is named more than 80 times, a bound that some block reaches. `segments`: within a row the ids never fall; a document holds at most 128 positions.
All inputs are finite; a program needn't handle non-finite values.
Results may differ from a plain program's by a relative error of at most 0.02.
The roundings to bfloat16 on the way count: a program that leaves them out, or rounds other values in their place, can miss the bound.
Values may be sent and summed in bfloat16 or wider, within the bound.
A program may use at most 384 MiB of HBM per device.

v0:
```python
import jax
import jax.numpy as jnp
from jax import lax
from jax.experimental import pallas as pl
from jax.experimental.pallas import tpu as pltpu
from jax.sharding import PartitionSpec as P


MODEL_WIDTH = 2048
HEAD_SIZE = 128
TOP = 8
SEQ = 256


EPS = 1e-06
THETA = 1000000.0
NEG = -1e30


def inverse_norm(value):
    return lax.rsqrt(jnp.mean(value * value, axis=-1, keepdims=True) + EPS)


def rotary_tables(sequence_length, width):
    half = width // 2
    inverse = THETA ** (-(jnp.arange(half).astype(jnp.float32) * 2.0 / width))
    angle = jnp.arange(sequence_length).astype(jnp.float32)[:, None] * inverse[None, :]
    return (jnp.cos(angle)[None, :, None, :], jnp.sin(angle)[None, :, None, :])


def row_norm_back(grad_normed, raw, rinv, gain):
    gain_grad = jnp.sum(grad_normed * raw * rinv, axis=0)
    scaled = grad_normed * gain
    grad_raw = rinv * scaled - raw * rinv**3 * jnp.mean(scaled * raw, axis=-1, keepdims=True)
    return (grad_raw, gain_grad)


def left_product(left, right):
    return lax.dot_general(
        left, right, (((0,), (0,)), ((), ())), preferred_element_type=jnp.float32
    )


def right_product(left, right):
    return lax.dot_general(
        left, right, (((1,), (1,)), ((), ())), preferred_element_type=jnp.float32
    )


ALL = ("fsdp", "expert")
WIDE = 512


def after(value, *earlier):
    return lax.optimization_barrier((value, *earlier))[0]


MESH = pl.DeviceIdType.MESH
MOST_VMEM = 62 * 1024 * 1024


def gather_kernel(ks, near, cap, place_ref, *refs):
    block_refs, out_refs = refs[: len(ks)], refs[len(ks) :]
    for i, (k, block_ref) in enumerate(zip(ks, block_refs)):
        for d in range(near):
            out_refs[d][i * cap : (i + 1) * cap, :] = jnp.dot(
                place_ref[k, d], block_ref[...], preferred_element_type=jnp.float32
            ).astype(jnp.bfloat16)


def gather_slots(place, ks, blocks):
    _, near, cap, count = place.shape
    width = blocks[0].shape[1]
    shape = jax.ShapeDtypeStruct((len(ks) * cap, width), jnp.bfloat16)
    return pl.pallas_call(
        lambda *refs: gather_kernel(ks, near, cap, *refs),
        in_specs=[whole_spec(place)] + [whole_spec(block) for block in blocks],
        out_specs=[whole_spec(shape)] * near,
        out_shape=[shape] * near,
        compiler_params=pltpu.CompilerParams(vmem_limit_bytes=MOST_VMEM),
        cost_estimate=pl.CostEstimate(
            flops=2 * len(ks) * near * cap * count * width,
            bytes_accessed=2 * len(ks) * width * (count + near * cap),
            transcendentals=0,
        ),
        name="gather_slots",
    )(place, *blocks)


def combine_kernel(spot_ref, gates_ref, *refs):
    piece_refs, out_ref = refs[:-1], refs[-1]
    total = None
    for d, piece_ref in enumerate(piece_refs):
        weight = spot_ref[0, d].astype(jnp.float32) * gates_ref[0][:, d : d + 1]
        high = weight.astype(jnp.bfloat16)
        for term in (high, (weight - high.astype(jnp.float32)).astype(jnp.bfloat16)):
            part = jnp.dot(term, piece_ref[...], preferred_element_type=jnp.float32)
            total = part if total is None else total + part
    out_ref[...] = total.astype(out_ref.dtype)


def combine_slots(spot, k, i, pieces, dtype, gates):
    _, near, count, cap = spot.shape
    width = pieces[0].shape[1]
    return pl.pallas_call(
        combine_kernel,
        grid=(width // WIDE,),
        in_specs=[
            pl.BlockSpec((1, near, count, cap), lambda j: (k, 0, 0, 0)),
            pl.BlockSpec((1, count, near), lambda j: (k, 0, 0)),
        ]
        + [pl.BlockSpec((cap, WIDE), lambda j: (i, j))] * near,
        out_specs=pl.BlockSpec((count, WIDE), lambda j: (0, j)),
        out_shape=jax.ShapeDtypeStruct((count, width), dtype),
        cost_estimate=pl.CostEstimate(
            flops=4 * near * cap * count * width,
            bytes_accessed=2 * width * (count + near * cap) + 2 * near * cap * count,
            transcendentals=0,
        ),
        name="combine_slots",
    )(spot, gates, *pieces)


class Place:
    def __init__(self, nf, nz):
        self.f, e = lax.axis_index("fsdp"), lax.axis_index("expert")
        self.z, self.c = e // 2, e % 2
        self.nf, self.nz = nf, nz

    def plane(self, k):
        return {"fsdp": self.f, "expert": lax.rem(self.z + k, self.nz) * 2 + self.c}

    def peer(self, d):
        df, dc = d // 2, d % 2
        core = 1 - self.c if dc else self.c
        return {"fsdp": self.flip(df), "expert": self.z * 2 + core}

    def flip(self, df):
        other, bit = 0, 1
        while bit < self.nf:
            digit = lax.rem(self.f // bit, 2)
            other = other + bit * (1 - digit if df & bit else digit)
            bit *= 2
        return other

    def greet(self):
        barrier = pltpu.get_barrier_semaphore()
        others = [self.plane(k) for k in range(1, self.nz)] + [self.peer(d) for d in range(1, 2 * self.nf)]
        for other in others:
            pl.semaphore_signal(barrier, inc=1, device_id=other, device_id_type=MESH)
        pl.semaphore_wait(barrier, len(others))


def remote(source, target, send, recv, device):
    return pltpu.make_async_remote_copy(
        src_ref=source, dst_ref=target, send_sem=send, recv_sem=recv, device_id=device, device_id_type=MESH
    )


def experts_kernel(
    nf, nz, cap, me_ref, place_ref, spot_ref, router_ref, block_ref, wg_any, wu_any, wd_any, *refs
):
    me = Place(nf, nz)
    near = 2 * nf
    early_refs, late_refs, refs = refs[:near], (None, *refs[near : near + nz - 1]), refs[near + nz - 1 :]
    own_ref, arrived_ref, blocks_ref, out_any, act_any, de_any, dgate_any, dup_any, back_ref, parts_ref, cots_ref = refs[:11]
    held, out, rows, cot, wg, wu, wd, de, act, dgate, dup, result, back, part, late, cot_out = refs[11:27]
    z_send, z_recv, sent, got, r_sent, r_got, p_send, p_recv, keep, loads, cot_loads, w_loads, stores, c_sent, c_got = refs[27:]
    width = rows.shape[1]
    tile = 256

    order = [*range(1, nz), 0]
    place_in = {k: i for i, k in enumerate(order)}

    def at(d):
        return pl.ds(d * cap, cap)

    def slot(k):
        return place_in[k] % 2

    def earlier(k, steps):
        return order[place_in[k] - steps] if place_in[k] >= steps else None

    def move(k):
        return remote(block_ref, held.at[k], z_send.at[k], z_recv.at[k], me.plane(k))

    def hop(k, d):
        there = arrived_ref.at[k, at(d)]
        if d == 0:
            return pltpu.make_async_copy(out.at[slot(k), at(d)], there, got.at[k, d])
        return remote(out.at[slot(k), at(d)], there, sent.at[k, d], got.at[k, d], me.peer(d))

    def hop_cot(k, d):
        there = cots_ref.at[k - 1, at(d)]
        if d == 0:
            return pltpu.make_async_copy(cot_out.at[slot(k), at(d)], there, c_got.at[k, d])
        return remote(cot_out.at[slot(k), at(d)], there, c_sent.at[k, d], c_got.at[k, d], me.peer(d))

    def load_cot(k):
        return pltpu.make_async_copy(late_refs[k], late, cot_loads.at[k, 0])

    def hop_back(k, d):
        there = back_ref.at[k, at(d)]
        if d == 0:
            return pltpu.make_async_copy(back.at[slot(k), at(d)], there, r_got.at[k, d])
        return remote(back.at[slot(k), at(d)], there, r_sent.at[k, d], r_got.at[k, d], me.peer(d))

    def along(k):
        return remote(
            part.at[k % 2], parts_ref.at[k - 1], p_send.at[k - 1], p_recv.at[k - 1], me.plane(nz - k)
        )

    def keep_block(k):
        return pltpu.make_async_copy(held.at[k], blocks_ref.at[k], keep.at[k])

    weights = [
        pltpu.make_async_copy(source.at[0], target, w_loads.at[i])
        for i, (source, target) in enumerate(((wg_any, wg), (wu_any, wu), (wd_any, wd)))
    ]
    own = pltpu.make_async_copy(block_ref, held.at[0], z_recv.at[0])

    def saves(k):
        pairs = ((result, out_any), (act, act_any), (de, de_any), (dgate, dgate_any), (dup, dup_any))
        return [pltpu.make_async_copy(source, target.at[k], stores.at[k, i]) for i, (source, target) in enumerate(pairs)]

    def gather(k):
        if k:
            move(k).wait_recv()
        else:
            own.wait()
        keep_block(k).start()
        if earlier(k, 2) is not None:
            for d in range(1, near):
                hop(earlier(k, 2), d).wait_send()
        for d in range(near):
            out[slot(k), at(d)] = jnp.dot(place_ref[k, d], held[k], preferred_element_type=jnp.float32).astype(
                jnp.bfloat16
            )
        for d in range(1, near):
            hop(k, d).start()
        hop(k, 0).start()

    def gather_cot(k):
        load_cot(k).wait()
        if k > 2:
            for d in range(1, near):
                hop_cot(k - 2, d).wait_send()
        for d in range(near):
            cot_out[slot(k), at(d)] = jnp.dot(place_ref[k, d], late[...], preferred_element_type=jnp.float32).astype(
                jnp.bfloat16
            )
        for d in range(1, near):
            hop_cot(k, d).start()
        hop_cot(k, 0).start()
        if k + 1 < nz:
            load_cot(k + 1).start()

    def expert(k):
        for d in range(near):
            hop(k, d).wait() if d == 0 else hop(k, d).wait_recv()
        load = pltpu.make_async_copy(arrived_ref.at[k], rows, loads.at[k])
        load.start()
        if k:
            for d in range(near):
                hop_cot(k, d).wait() if d == 0 else hop_cot(k, d).wait_recv()
            cot_moves = [
                pltpu.make_async_copy(cots_ref.at[k - 1], cot.at[:, pl.ds(0, late.shape[1])], cot_loads.at[k, 1])
            ]
        else:
            cot_moves = [
                pltpu.make_async_copy(early_refs[d], cot.at[at(d), pl.ds(0, late.shape[1])], cot_loads.at[0, d])
                for d in range(near)
            ]
        for one in cot_moves:
            one.start()
        if earlier(k, 1) is not None:
            for one in saves(earlier(k, 1)):
                one.wait()
        else:
            for one in weights:
                one.wait()
        load.wait()
        for one in cot_moves:
            one.wait()
        for d in range(near):
            span = at(d)
            logits = jnp.dot(rows[span, :], router_ref[...], preferred_element_type=jnp.float32)
            picked = cot[span, width : width + logits.shape[1]].astype(jnp.float32) > 0.5
            highest = jnp.max(jnp.where(picked, logits, NEG), axis=-1, keepdims=True)
            raised = jnp.exp(jnp.where(picked, logits - highest, NEG))
            lane = lax.broadcasted_iota(jnp.int32, logits.shape, 1)
            mine = jnp.sum(jnp.where(lane == me_ref[0], raised, 0.0), axis=-1, keepdims=True)
            gate = mine / jnp.maximum(jnp.sum(raised, axis=-1, keepdims=True), 1e-30)
            de[span, :] = (gate * cot[span, :width].astype(jnp.float32)).astype(jnp.bfloat16)

        def hidden(j, _):
            cols = pl.ds(pl.multiple_of(j * tile, tile), tile)
            gate_pre = jnp.dot(rows[...], wg[:, cols], preferred_element_type=jnp.float32)
            up_pre = jnp.dot(rows[...], wu[:, cols], preferred_element_type=jnp.float32)
            sigma = jax.nn.sigmoid(gate_pre)
            act[:, cols] = (gate_pre * sigma * up_pre).astype(jnp.bfloat16)
            d_act = right_product(de[...], wd[cols, :])
            dgate[:, cols] = (d_act * up_pre * sigma * (1.0 + gate_pre * (1.0 - sigma))).astype(jnp.bfloat16)
            dup[:, cols] = (d_act * gate_pre * sigma).astype(jnp.bfloat16)
            return 0

        lax.fori_loop(0, act.shape[1] // tile, hidden, 0)
        if earlier(k, 2) is not None:
            for d in range(1, near):
                hop_back(earlier(k, 2), d).wait_send()

        def model(n, rest):
            cols = pl.ds(pl.multiple_of(n * tile, tile), tile)
            result[:, cols] = jnp.dot(act[...], wd[:, cols], preferred_element_type=jnp.float32).astype(jnp.bfloat16)
            d_rows = right_product(dgate[...], wg[cols, :]) + right_product(dup[...], wu[cols, :])
            back[slot(k), :, cols] = d_rows.astype(jnp.bfloat16)
            return rest + jnp.sum(
                cot[:, cols].astype(jnp.float32) * result[:, cols].astype(jnp.float32), axis=-1, keepdims=True
            )

        rest = lax.fori_loop(0, width // tile, model, jnp.zeros((near * cap, 1), jnp.float32))
        shape = (near * cap, back.shape[2] - width)
        lane = lax.broadcasted_iota(jnp.int32, shape, 1) - (lax.broadcasted_iota(jnp.int32, shape, 0) // cap + k * near) * 3
        extra = jnp.zeros(shape, jnp.float32)
        for i in range(3):
            term = rest.astype(jnp.bfloat16).astype(jnp.float32)
            extra = jnp.where(lane == i, term, extra)
            rest = rest - term
        back[slot(k), :, width:] = extra.astype(jnp.bfloat16)
        for d in range(1, near):
            hop_back(k, d).start()
        hop_back(k, 0).start()
        for one in saves(k):
            one.start()

    def combine(k):
        for d in range(near):
            hop_back(k, d).wait() if d == 0 else hop_back(k, d).wait_recv()
        load = pltpu.make_async_copy(back_ref.at[k], cot.at[:, pl.ds(0, back.shape[2])], loads.at[nz + k])
        load.start()
        load.wait()
        for d in range(near):
            term = jnp.dot(spot_ref[k, d], cot[at(d), : back.shape[2]], preferred_element_type=jnp.float32)
            if d:
                own_ref[...] += term
            else:
                own_ref[...] = term
        if k:
            if k > 2:
                along(k - 2).wait_send()
            part[k % 2] = own_ref[...].astype(jnp.bfloat16)
            along(k).start()

    for one in weights:
        one.start()
    me.greet()
    for k in range(1, nz):
        move(k).start()
    own.start()
    load_cot(1).start()
    gather_cot(1)
    gather(1)
    for k in range(1, nz):
        if k + 1 < nz:
            gather_cot(k + 1)
        if k == 1:
            expert(k)
        if k + 1 < nz:
            gather(k + 1)
        else:
            gather(0)
        if k > 1:
            combine(k - 1)
            expert(k)
    combine(nz - 1)
    expert(0)
    combine(0)
    for k in range(nz):
        keep_block(k).wait()
        if k:
            move(k).wait_send()
            if k >= nz - 2:
                along(k).wait_send()
            along(k).wait_recv()
    for k in order[-2:]:
        for d in range(1, near):
            hop(k, d).wait_send()
            hop_back(k, d).wait_send()
    for k in (nz - 2, nz - 1):
        for d in range(1, near):
            hop_cot(k, d).wait_send()
    for one in saves(order[-1]):
        one.wait()


def run_experts(nf, me, place, spot, router, block, w_gate, w_up, w_down, early, late):
    nz, near, cap, count = place.shape
    width, hidden = w_gate.shape[1:]
    rows = near * cap
    extra = -(-3 * near * nz // 128) * 128
    wide = max(width + extra, early[0].shape[1])
    low = jnp.bfloat16
    anywhere = pl.BlockSpec(memory_space=pl.ANY)
    own = jax.ShapeDtypeStruct((count, width + extra), jnp.float32)
    shapes = [
        jax.ShapeDtypeStruct(shape, low)
        for shape in (
            (nz, rows, width),
            (nz, count, width),
            (nz, rows, width),
            (nz, rows, hidden),
            (nz, rows, width),
            (nz, rows, hidden),
            (nz, rows, hidden),
            (nz, rows, width + extra),
            (nz - 1, count, width + extra),
            (nz - 1, rows, early[0].shape[1]),
        )
    ]
    dma = pltpu.SemaphoreType.DMA
    return pl.pallas_call(
        lambda *refs: experts_kernel(nf, nz, cap, *refs),
        in_specs=[SCALARS, whole_spec(place), whole_spec(spot), whole_spec(router)] + [anywhere] * (4 + near + len(late)),
        out_specs=[whole_spec(own)] + [anywhere] * len(shapes),
        out_shape=[own] + shapes,
        scratch_shapes=[
            pltpu.VMEM((nz, count, width), low),
            pltpu.VMEM((2, rows, width), low),
            pltpu.VMEM((rows, width), low),
            pltpu.VMEM((rows, wide), low),
            pltpu.VMEM((width, hidden), low),
            pltpu.VMEM((width, hidden), low),
            pltpu.VMEM((hidden, width), low),
            pltpu.VMEM((rows, width), low),
            pltpu.VMEM((rows, hidden), low),
            pltpu.VMEM((rows, hidden), low),
            pltpu.VMEM((rows, hidden), low),
            pltpu.VMEM((rows, width), low),
            pltpu.VMEM((2, rows, width + extra), low),
            pltpu.VMEM((2, count, width + extra), low),
            pltpu.VMEM((count, early[0].shape[1]), low),
            pltpu.VMEM((2, rows, early[0].shape[1]), low),
            dma((nz,)),
            dma((nz,)),
            dma((nz, near)),
            dma((nz, near)),
            dma((nz, near)),
            dma((nz, near)),
            dma((nz - 1,)),
            dma((nz - 1,)),
            dma((nz,)),
            dma((2 * nz,)),
            dma((nz, near)),
            dma((3,)),
            dma((nz, 5)),
            dma((nz, near)),
            dma((nz, near)),
        ],
        compiler_params=pltpu.CompilerParams(collective_id=0, has_side_effects=True, vmem_limit_bytes=MOST_VMEM),
        cost_estimate=pl.CostEstimate(
            flops=12 * nz * rows * width * hidden, bytes_accessed=600_000_000, transcendentals=0
        ),
        name="run_experts",
    )(me, place, spot, router, block, w_gate, w_up, w_down, *early, *late)


def whole_spec(value):
    return pl.BlockSpec(value.shape, lambda *_: (0,) * len(value.shape))


SCALARS = pl.BlockSpec(memory_space=pltpu.SMEM)


def scores_of(q_rot, k_rot, seg_col, seg_row):
    scores = right_product(q_rot, k_rot) * HEAD_SIZE ** (-0.5)
    here = lax.broadcasted_iota(jnp.int32, scores.shape, 0) >= lax.broadcasted_iota(jnp.int32, scores.shape, 1)
    return jnp.where(here & (seg_col == seg_row), scores, NEG)


def turn(value, cos, sin):
    return value * cos + pltpu.roll(value, HEAD_SIZE // 2, 1) * sin


def attend_kernel(blocks, heads, kv_heads, spots, x_ref, gain_ref, row_ref, col_ref, cos_ref, sin_ref, qg_ref, kg_ref, *refs):
    w_refs, refs = refs[:blocks], refs[blocks:]
    normed_ref, raw_ref, rot_ref, value_ref, mixed_ref, lse_ref = refs
    wide = x_ref[...].astype(jnp.float32)
    normed_ref[...] = (wide * inverse_norm(wide) * gain_ref[...]).astype(jnp.bfloat16)
    depth = w_refs[0].shape[0]
    total = None
    for i, w_ref in enumerate(w_refs):
        part = normed_ref[...] if blocks == 1 else normed_ref[:, pl.ds(pl.multiple_of(spots[i] * depth, depth), depth)]
        part = jnp.dot(part, w_ref[...], preferred_element_type=jnp.float32)
        total = part if total is None else total + part
    turned = (heads + kv_heads) * HEAD_SIZE
    raw_ref[...] = total[:, :turned]
    value_ref[...] = total[:, turned:].astype(jnp.bfloat16)
    cos, sin = cos_ref[...], sin_ref[...]
    for h in range(heads + kv_heads):
        at = slice(h * HEAD_SIZE, (h + 1) * HEAD_SIZE)
        raw = raw_ref[:, at]
        gain = qg_ref[...] if h < heads else kg_ref[...]
        rot_ref[:, at] = turn(raw * inverse_norm(raw) * gain, cos, sin).astype(jnp.bfloat16)
    lane = lax.broadcasted_iota(jnp.int32, lse_ref.shape, 1)
    all_lse = jnp.zeros(lse_ref.shape, jnp.float32)
    for h in range(heads):
        at = slice(h * HEAD_SIZE, (h + 1) * HEAD_SIZE)
        g = h * kv_heads // heads
        masked = scores_of(
            rot_ref[:, at],
            rot_ref[:, (heads + g) * HEAD_SIZE : (heads + g + 1) * HEAD_SIZE],
            col_ref[...],
            row_ref[...],
        )
        top = jnp.max(masked, axis=-1, keepdims=True)
        lse = top + jnp.log(jnp.sum(jnp.exp(masked - top), axis=-1, keepdims=True))
        prob_low = jnp.exp(masked - lse).astype(jnp.bfloat16)
        mixed_ref[:, at] = jnp.dot(
            prob_low, value_ref[:, g * HEAD_SIZE : (g + 1) * HEAD_SIZE], preferred_element_type=jnp.float32
        ).astype(jnp.bfloat16)
        all_lse = jnp.where(lane == h, lse, all_lse)
    lse_ref[...] = all_lse


def attend(spots, tokens, gain, seg_row, seg_col, cos, sin, qg, kg, w_blocks, heads, kv_heads):
    count, width = tokens.shape
    args = (tokens, gain, seg_row, seg_col, cos, sin, qg, kg, *w_blocks)
    shapes = [
        jax.ShapeDtypeStruct((count, width), jnp.bfloat16),
        jax.ShapeDtypeStruct((count, (heads + kv_heads) * HEAD_SIZE), jnp.float32),
        jax.ShapeDtypeStruct((count, (heads + kv_heads) * HEAD_SIZE), jnp.bfloat16),
        jax.ShapeDtypeStruct((count, kv_heads * HEAD_SIZE), jnp.bfloat16),
        jax.ShapeDtypeStruct((count, heads * HEAD_SIZE), jnp.bfloat16),
        jax.ShapeDtypeStruct((count, 128), jnp.float32),
    ]
    return pl.pallas_call(
        lambda *refs: attend_kernel(len(w_blocks), heads, kv_heads, *refs),
        in_specs=[SCALARS] + [whole_spec(v) for v in args],
        out_specs=[whole_spec(v) for v in shapes],
        out_shape=shapes,
        cost_estimate=pl.CostEstimate(
            flops=2 * count * width * (heads + 2 * kv_heads) * HEAD_SIZE + 4 * heads * count * count * HEAD_SIZE,
            bytes_accessed=2 * width * (heads + 2 * kv_heads) * HEAD_SIZE + 16 * count * width,
            transcendentals=2 * heads * count * count,
        ),
        name="attend",
    )(spots, *args)


def project_kernel(blocks, spots, mixed_ref, *refs):
    w_refs, out_ref = refs[:blocks], refs[-1]
    depth = w_refs[0].shape[0]
    total = None
    for i, w_ref in enumerate(w_refs):
        part = mixed_ref[...] if blocks == 1 else mixed_ref[:, pl.ds(pl.multiple_of(spots[i] * depth, depth), depth)]
        part = jnp.dot(part, w_ref[...], preferred_element_type=jnp.float32)
        total = part if total is None else total + part
    out_ref[...] = total.astype(out_ref.dtype)


def project(spots, mixed, w_blocks, dtype):
    count, depth = mixed.shape
    width = w_blocks[0].shape[1]
    return pl.pallas_call(
        lambda *refs: project_kernel(len(w_blocks), *refs),
        grid=(width // WIDE,),
        in_specs=[SCALARS, pl.BlockSpec((count, depth), lambda j: (0, 0))]
        + [pl.BlockSpec((w.shape[0], WIDE), lambda j: (0, j)) for w in w_blocks],
        out_specs=pl.BlockSpec((count, WIDE), lambda j: (0, j)),
        out_shape=jax.ShapeDtypeStruct((count, width), dtype),
        cost_estimate=pl.CostEstimate(
            flops=2 * count * depth * width, bytes_accessed=2 * depth * width + 4 * count * width, transcendentals=0
        ),
        name="project",
    )(spots, mixed, *w_blocks)


def head_back(grad_rot, raw, gain, cos, sin):
    grad_normed = turn(grad_rot, cos, -sin)
    rinv = inverse_norm(raw)
    gain_grad = jnp.sum(grad_normed * raw * rinv, axis=0, keepdims=True)
    scaled = grad_normed * gain
    return rinv * scaled - raw * rinv**3 * jnp.mean(scaled * raw, axis=-1, keepdims=True), gain_grad


def attend_back_kernel(
    blocks, heads, kv_heads, spots, dmid_ref, x_ref, row_ref, col_ref, cos_ref, sin_ref, qg_ref, kg_ref,
    raw_ref, rot_ref, value_ref, mixed_ref, lse_ref, *refs
):
    o_refs, w_refs, refs = refs[:blocks], refs[blocks : 2 * blocks], refs[2 * blocks :]
    dheads_ref, part_ref, gain_ref, qgain_ref, kgain_ref, dmixed = refs
    scale = HEAD_SIZE ** (-0.5)
    dmid = dmid_ref[...]
    depth = o_refs[0].shape[0]
    for i, o_ref in enumerate(o_refs):
        part = right_product(dmid, o_ref[...]).astype(jnp.bfloat16)
        if blocks == 1:
            dmixed[...] = part
        else:
            dmixed[:, pl.ds(pl.multiple_of(spots[i] * depth, depth), depth)] = part
    cos, sin = cos_ref[...], sin_ref[...]
    lane = lax.broadcasted_iota(jnp.int32, lse_ref.shape, 1)
    all_lse = lse_ref[...]
    q_gain = jnp.zeros(qgain_ref.shape, jnp.float32)
    k_gain = jnp.zeros(kgain_ref.shape, jnp.float32)
    for g in range(kv_heads):
        kv = slice(g * HEAD_SIZE, (g + 1) * HEAD_SIZE)
        key_at = slice((heads + g) * HEAD_SIZE, (heads + g + 1) * HEAD_SIZE)
        k_rot, value = rot_ref[:, key_at], value_ref[:, kv]
        d_value, d_key = None, None
        for h in range(g * heads // kv_heads, (g + 1) * heads // kv_heads):
            at = slice(h * HEAD_SIZE, (h + 1) * HEAD_SIZE)
            q_rot, grad = rot_ref[:, at], dmixed[:, at]
            lse = jnp.sum(jnp.where(lane == h, all_lse, 0.0), axis=-1, keepdims=True)
            prob = jnp.exp(scores_of(q_rot, k_rot, col_ref[...], row_ref[...]) - lse)
            part = left_product(prob.astype(jnp.bfloat16), grad)
            d_value = part if d_value is None else d_value + part
            d_prob = right_product(grad, value)
            delta = jnp.sum(grad.astype(jnp.float32) * mixed_ref[:, at].astype(jnp.float32), axis=-1, keepdims=True)
            d_scores = (prob * (d_prob - delta)).astype(jnp.bfloat16)
            part = left_product(d_scores, q_rot)
            d_key = part if d_key is None else d_key + part
            d_q = jnp.dot(d_scores, k_rot, preferred_element_type=jnp.float32) * scale
            d_query, gain_part = head_back(d_q, raw_ref[:, at], qg_ref[...], cos, sin)
            q_gain = q_gain + gain_part
            dheads_ref[:, at] = d_query.astype(jnp.bfloat16)
        d_key, gain_part = head_back(d_key * scale, raw_ref[:, key_at], kg_ref[...], cos, sin)
        k_gain = k_gain + gain_part
        dheads_ref[:, key_at] = d_key.astype(jnp.bfloat16)
        last = (heads + kv_heads + g) * HEAD_SIZE
        dheads_ref[:, last : last + HEAD_SIZE] = d_value.astype(jnp.bfloat16)
    qgain_ref[...] = q_gain
    kgain_ref[...] = k_gain
    d_heads = dheads_ref[...]
    wide = x_ref[...].astype(jnp.float32)
    rinv = inverse_norm(wide)
    depth = w_refs[0].shape[0]
    for i, w_ref in enumerate(w_refs):
        part = right_product(d_heads, w_ref[...])
        at = slice(None) if blocks == 1 else pl.ds(pl.multiple_of(spots[i] * depth, depth), depth)
        part_ref[:, at] = part.astype(part_ref.dtype)
        x = x_ref[:, at].astype(jnp.float32)
        gain_ref[:, at] = jnp.sum(part * x * rinv, axis=0, keepdims=True)


def attend_back(spots, dmid, tokens, seg_row, seg_col, cos, sin, qg, kg, saved, o_blocks, w_blocks, heads, kv_heads, dtype):
    count, width = tokens.shape
    args = (dmid, tokens, seg_row, seg_col, cos, sin, qg, kg, *saved, *o_blocks, *w_blocks)
    lanes = (heads + 2 * kv_heads) * HEAD_SIZE
    shapes = [
        jax.ShapeDtypeStruct((count, lanes), jnp.bfloat16),
        jax.ShapeDtypeStruct((count, width), dtype),
        jax.ShapeDtypeStruct((1, width), jnp.float32),
        jax.ShapeDtypeStruct((1, HEAD_SIZE), jnp.float32),
        jax.ShapeDtypeStruct((1, HEAD_SIZE), jnp.float32),
    ]
    return pl.pallas_call(
        lambda *refs: attend_back_kernel(len(w_blocks), heads, kv_heads, *refs),
        in_specs=[SCALARS] + [whole_spec(v) for v in args],
        out_specs=[whole_spec(v) for v in shapes],
        out_shape=shapes,
        scratch_shapes=[pltpu.VMEM((count, heads * HEAD_SIZE), jnp.bfloat16)],
        cost_estimate=pl.CostEstimate(
            flops=4 * count * width * lanes + 10 * heads * count * count * HEAD_SIZE,
            bytes_accessed=4 * width * lanes + 24 * count * width,
            transcendentals=heads * count * count,
        ),
        name="attend_back",
    )(spots, *args)


def on_device(
    tokens,
    segments,
    routes,
    attn_gain,
    w_query,
    key_matrix,
    value_matrix,
    output_matrix,
    query_gain,
    key_gain,
    ffn_gain,
    w_router,
    w_gate,
    w_up,
    w_down,
    cotangent,
):
    nf, ne = lax.axis_size("fsdp"), lax.axis_size("expert")
    nz = ne // 2
    f, e = lax.axis_index("fsdp"), lax.axis_index("expert")
    z, c = e // 2, e % 2
    count = tokens.shape[0]
    experts = nf * ne
    cap = -(5 * count * TOP // (4 * experts)) // 16 * -16
    peers = [(df, dc) for df in range(nf) for dc in range(2)]
    near = len(peers)

    def across(value, df, dc):
        return lax.ppermute(
            value, ALL, [(i * ne + j, (i ^ df) * ne + (j ^ dc)) for i in range(nf) for j in range(ne)]
        )

    def along(value, k):
        return lax.ppermute(value, "expert", [(j, (j + 2 * k) % ne) for j in range(ne)])

    def group_blocks(value):
        return [value] + [across(value, df, 0) for df in range(1, nf)]

    def plane_blocks(value):
        blocks = [value]
        for k in range(1, nz):
            blocks.append(along(value, k))
        return blocks

    def spread_rows(blocks):
        rows, width = blocks[0].shape
        places, pieces = [], []
        for k, block in enumerate(blocks):
            places += [(z - k) % nz * 2 + c, (z - k) % nz * 2 + 1 - c]
            pieces += [block, across(block, 0, 1)]
        if rows % 128 == 0:
            return pieces, jnp.stack(places).astype(jnp.int32)
        whole = jnp.zeros((ne, rows, width), blocks[0].dtype)
        for at, piece in zip(places, pieces):
            whole = lax.dynamic_update_slice(whole, piece[None], (at, 0, 0))
        return [whole.reshape(ne * rows, width)], jnp.zeros((1,), jnp.int32)

    def reduce_rows(grad):
        grad = grad.reshape(nz, 2, grad.shape[0] // ne, grad.shape[1])
        theirs = lax.dynamic_index_in_dim(grad, 1 - c, 1, keepdims=False).astype(jnp.bfloat16)
        mine = lax.dynamic_index_in_dim(grad, c, 1, keepdims=False)
        mine = mine + across(theirs, 0, 1).astype(jnp.float32)
        total = lax.dynamic_index_in_dim(mine, z, 0, keepdims=False)
        parts = [lax.dynamic_index_in_dim(mine, (z + k) % nz, 0, keepdims=False) for k in range(1, nz)]
        parts = [part.astype(jnp.bfloat16) for part in parts]
        for k, part in enumerate(parts, 1):
            total = total + along(part, k).astype(jnp.float32)
        return total, parts

    def add_pairs(values):
        while len(values) > 1:
            values = [a + b for a, b in zip(values[::2], values[1::2])]
        return values[0]

    def sum_small(columns, row, *earlier):
        blocks = columns.reshape(nz, 2, MODEL_WIDTH // ne, columns.shape[1])
        rows = jnp.broadcast_to(row[None, None], (nz, 2) + row.shape)
        blocks = jnp.concatenate([blocks, rows], axis=2)
        mine = lax.dynamic_index_in_dim(blocks, c, 1, keepdims=False)
        mine = mine + across(lax.dynamic_index_in_dim(blocks, 1 - c, 1, keepdims=False), 0, 1)
        mine = after(mine, *earlier)
        sends = [lax.dynamic_index_in_dim(mine, z ^ step, 0, keepdims=False) for step in range(nz)]
        pairs = [[(j, j ^ (2 * step)) for j in range(ne)] for step in range(nz)]
        return add_pairs([lax.ppermute(v, "expert", p) if i else v for i, (v, p) in enumerate(zip(sends, pairs))])

    width_q, width_k = w_query.shape[1], key_matrix.shape[1]
    w_heads = jnp.concatenate([w_query, key_matrix, value_matrix], axis=1)
    token_blocks = group_blocks(tokens)
    segment_blocks = group_blocks(segments)
    few = jnp.concatenate(
        [jnp.transpose(routes).astype(jnp.bfloat16).reshape(-1, w_router.shape[0]), attn_gain[None], ffn_gain[None], jnp.transpose(w_router)]
    )
    few_blocks = plane_blocks(few)
    heads_blocks = plane_blocks(after(w_heads, few))
    few_pairs = across(jnp.stack([block[-experts - 2 :] for block in few_blocks]), 0, 1)
    few_whole = jnp.zeros((nz, 2) + few_pairs.shape[1:], jnp.bfloat16)
    for k, block in enumerate(few_blocks):
        for core, piece in ((c, block[-experts - 2 :]), (1 - c, few_pairs[k])):
            few_whole = lax.dynamic_update_slice(few_whole, piece[None, None], ((z - k) % nz, core, 0, 0))
    few_whole = jnp.transpose(few_whole, (2, 0, 1, 3)).reshape(experts + 2, MODEL_WIDTH)
    gain_one, gain_two = few_whole[:1].astype(jnp.float32), few_whole[1:2].astype(jnp.float32)
    full_router = jnp.transpose(jnp.pad(few_whole[2:], ((0, -experts % 128), (0, 0))))
    route_blocks = [block[: -experts - 2].reshape(TOP, count).astype(jnp.int32) for block in few_blocks]
    picked = jnp.any(routes[:, :, None] == jnp.arange(full_router.shape[1])[None, None, :], axis=1)
    cot_wide = jnp.concatenate([cotangent, picked.astype(jnp.bfloat16)], axis=1)

    peer_experts = jnp.stack([(f ^ df) * ne + 2 * z + (c ^ dc) for df, dc in peers])
    named = jnp.stack(route_blocks)
    hit = jnp.any(named[:, None] == peer_experts[None, :, None, None], axis=2)
    upto = (jnp.arange(count)[:, None] <= jnp.arange(count)[None, :]).astype(jnp.bfloat16)
    rank = jnp.dot(
        hit.astype(jnp.bfloat16).reshape(nz * near, count), upto, preferred_element_type=jnp.float32
    ).reshape(nz, near, count)
    slot_of = jnp.where(hit, rank - 1.0, -1.0)
    slots = jnp.arange(cap, dtype=jnp.float32)
    place = (slot_of[:, :, None, :] == slots[None, None, :, None]).astype(jnp.bfloat16)
    spot = (slot_of[:, :, :, None] == slots[None, None, None, :]).astype(jnp.bfloat16)

    def send_out(pieces):
        got = [pieces[0]]
        for d, (df, dc) in enumerate(peers[1:], 1):
            got.append(across(pieces[d], df, dc))
        return got

    early = send_out(gather_slots(place, (0,), [after(cot_wide, *token_blocks[1:])]))

    local_q = width_q // HEAD_SIZE
    local_kv = width_k // HEAD_SIZE
    w_blocks, spots = spread_rows([after(block, few_whole) for block in heads_blocks])
    head_blocks = plane_blocks(after(output_matrix, *w_blocks))
    cot_blocks = plane_blocks(after(cot_wide, *w_blocks))
    cosine, sine = rotary_tables(SEQ, HEAD_SIZE)
    cos = jnp.concatenate([cosine[0, :, 0], cosine[0, :, 0]], axis=-1)
    sin = jnp.concatenate([-sine[0, :, 0], sine[0, :, 0]], axis=-1)
    q_scale = query_gain.astype(jnp.float32)[None]
    k_scale = key_gain.astype(jnp.float32)[None]
    turns = [1 + df for df in range(nf - 1)] + [0]
    shared = [
        (segment_blocks[df], jnp.transpose(segment_blocks[df]), cos, sin, q_scale, k_scale) for df in range(nf)
    ]
    attended = [None] * nf
    for turn_at, df in enumerate(turns):
        attended[df] = attend(
            spots,
            after(token_blocks[df], *([attended[turns[turn_at - 1]][4]] if turn_at else [])),
            gain_one,
            *shared[df],
            w_blocks,
            local_q,
            local_kv,
        )
    o_blocks, _ = spread_rows([after(block, attended[turns[-2]][0]) for block in head_blocks])
    wide_in = tokens.astype(jnp.float32)
    rinv_one = inverse_norm(wide_in)
    residual_mid = wide_in
    for df in turns:
        part = project(spots, attended[df][4], o_blocks, jnp.bfloat16 if df else jnp.float32)
        if df:
            part = across(part, df, 0).astype(jnp.float32)
        residual_mid = residual_mid + part

    rinv_two = inverse_norm(residual_mid)
    normed_two = (residual_mid * rinv_two * gain_two).astype(jnp.bfloat16)
    me = (f * ne + e).astype(jnp.int32)[None]
    own_sum, arrived, normed_blocks, expert_out, act, d_expert, d_gate_pre, d_up_pre, _, plane_sums, _ = run_experts(
        nf, me, place, spot, full_router, normed_two, w_gate, w_up, w_down, early, cot_blocks[1:]
    )
    back_sum = own_sum + jnp.sum(plane_sums.astype(jnp.float32), axis=0)
    d_normed_two = back_sum[:, :MODEL_WIDTH]

    def gates_of(rows, named_rows):
        logits = jnp.dot(rows, full_router, preferred_element_type=jnp.float32)[:, :experts]
        picked = jnp.any(named_rows[:, :, None] == jnp.arange(experts)[None, None, :], axis=0)
        highest = jnp.max(jnp.where(picked, logits, NEG), axis=-1, keepdims=True)
        raised = jnp.where(picked, jnp.exp(jnp.minimum(logits - highest, 0.0)), 0.0)
        return raised / jnp.sum(raised, axis=-1, keepdims=True)

    gates = gates_of(normed_two, route_blocks[0])

    owners = jnp.concatenate(
        [jnp.repeat(peer_experts + 2 * ((z + k) % nz - z), 3) for k in range(nz)]
    )
    names = (owners[:, None] == jnp.arange(experts)[None, :]).astype(jnp.float32)
    d_gates = jnp.dot(
        back_sum[:, MODEL_WIDTH : MODEL_WIDTH + 3 * near * nz], names, precision=lax.Precision.HIGHEST
    )
    d_logits = (gates * (d_gates - jnp.sum(gates * d_gates, axis=-1, keepdims=True))).astype(jnp.bfloat16)

    router_grad = left_product(normed_two, d_logits)
    d_normed_two = d_normed_two + right_product(d_logits, full_router[:, :experts])
    d_norm_part, gain_two_grad = row_norm_back(d_normed_two, residual_mid, rinv_two, gain_two)
    d_mid = cotangent.astype(jnp.float32) + d_norm_part
    middle_blocks = group_blocks(d_mid.astype(jnp.bfloat16))
    arrived, act, d_expert, d_gate_pre, d_up_pre = after(
        tuple(
            value.reshape(nz * near * cap, value.shape[2])
            for value in (arrived, act, d_expert, d_gate_pre, d_up_pre)
        ),
        middle_blocks[0],
    )
    down_grad = left_product(act, d_expert)
    gate_grad = left_product(arrived, d_gate_pre)
    up_grad = left_product(arrived, d_up_pre)

    is_peer = peer_experts[None, :, None] == jnp.arange(experts)[None, None, :]
    peer_gates = jnp.stack(
        [
            jnp.sum(jnp.where(is_peer, gates_of(normed_blocks[k], route_blocks[k])[:, None, :], 0.0), axis=-1)
            for k in range(nz)
        ]
    )
    expert_out = after(expert_out, *middle_blocks[1:])
    groups = [list(range(1, nz // 2 + 1)), list(range(nz // 2 + 1, nz)) + [0]]
    come = {}
    for group in groups:
        pieces = [
            jnp.concatenate([expert_out[k, d * cap : (d + 1) * cap] for k in group], axis=0) for d in range(near)
        ]
        pieces = send_out(pieces)
        for i, k in enumerate(group):
            come[k] = (i, pieces)

    home_parts = {}

    def home_sum(k, weights):
        part = combine_slots(spot, k, *come[k], jnp.bfloat16 if k else jnp.float32, weights)
        home_parts[k] = part
        if k:
            part = along(part, nz - k).astype(jnp.float32)
        return part

    mixed = jnp.concatenate([attended[df][4] for df in range(nf)], axis=0)
    share_out, out_parts = reduce_rows(left_product(mixed, jnp.concatenate(middle_blocks, axis=0)))
    moe = [home_sum(k, after(peer_gates, *out_parts)) for k in groups[0]]
    d_heads = [None] * nf
    d_normed_one, gain_one_grad, q_gain_grad, k_gain_grad = None, None, None, None
    for df in range(nf):
        d_heads[df], part, *sums = attend_back(
            spots,
            after(
                middle_blocks[df],
                *([d_heads[df - 1]] if df else []),
                *([home_parts[k] for k in groups[0]] if df == nf - 1 else []),
            ),
            token_blocks[df],
            *shared[df],
            attended[df][1:],
            o_blocks,
            w_blocks,
            local_q,
            local_kv,
            jnp.bfloat16 if df else jnp.float32,
        )
        if df:
            part = across(part, df, 0).astype(jnp.float32)
            d_normed_one = d_normed_one + part
            gain_one_grad, q_gain_grad, k_gain_grad = [
                a + b for a, b in zip((gain_one_grad, q_gain_grad, k_gain_grad), sums)
            ]
        else:
            d_normed_one = part
            gain_one_grad, q_gain_grad, k_gain_grad = sums
    normed_one = jnp.concatenate([attended[df][0] for df in range(nf)], axis=0)
    share_heads, head_parts = reduce_rows(left_product(normed_one, jnp.concatenate(d_heads, axis=0)))
    columns = jnp.concatenate([router_grad, jnp.transpose(gain_one_grad), gain_two_grad[:, None]], axis=1)
    columns = jnp.pad(columns, ((0, 0), (0, -columns.shape[1] % 128)))
    row = jnp.pad(jnp.concatenate([q_gain_grad, k_gain_grad]), ((0, 6), (0, columns.shape[1] - HEAD_SIZE)))
    small = sum_small(columns, row, *head_parts)
    for k in groups[1]:
        moe.append(home_sum(k, after(peer_gates, *head_parts)))
    moe = sum(moe[1:], moe[0])
    output = (residual_mid + moe).astype(jnp.bfloat16)
    small = after(small, home_parts[0])
    small = add_pairs([across(small, df, 0) if df else small for df in range(nf)])

    d_tokens, _ = row_norm_back(d_normed_one, wide_in, rinv_one, gain_one)
    token_grad = d_mid + d_tokens

    rows_own = MODEL_WIDTH // ne
    return (
        output,
        token_grad,
        small[:rows_own, experts],
        share_heads[:, :width_q],
        share_heads[:, width_q : width_q + width_k],
        share_heads[:, width_q + width_k :],
        share_out,
        small[rows_own, :HEAD_SIZE],
        small[rows_own + 1, :HEAD_SIZE],
        small[:rows_own, experts + 1],
        small[:rows_own, :experts],
        gate_grad[None],
        up_grad[None],
        down_grad[None],
    )


def solution(mesh):
    return jax.shard_map(
        on_device,
        mesh=mesh,
        in_specs=(
            P(("fsdp", "expert"), None),
            P(("fsdp", "expert"), None),
            P(("fsdp", "expert"), None),
            P("expert"),
            P("expert", "fsdp"),
            P("expert", "fsdp"),
            P("expert", "fsdp"),
            P(("fsdp", "expert"), None),
            P(),
            P(),
            P("expert"),
            P("expert", None),
            P(("fsdp", "expert"), None, None),
            P(("fsdp", "expert"), None, None),
            P(("fsdp", "expert"), None, None),
            P(("fsdp", "expert"), None),
        ),
        out_specs=(
            P(("fsdp", "expert"), None),
            P(("fsdp", "expert"), None),
            P("expert"),
            P("expert", "fsdp"),
            P("expert", "fsdp"),
            P("expert", "fsdp"),
            P(("fsdp", "expert"), None),
            P(),
            P(),
            P("expert"),
            P("expert", None),
            P(("fsdp", "expert"), None, None),
            P(("fsdp", "expert"), None, None),
            P(("fsdp", "expert"), None, None),
        ),
        check_vma=False,
    )
```

profile of v0, /device:TPU:21, one launch (start us, length us, event | category | flops | bytes accessed | tf_op | source)
XLA Modules:
  0.0 1215.9 jit_solution(12386618287260848462)
XLA Ops:
  28.9 7.5 collective-permute-done.9.refs_13_.refs_26_
  36.4 5.2 collective-permute-start.6
  74.4 12.2 collective-permute-start.22
  95.4 10.8 attend.4
  106.2 6.9 collective-permute-done.14.refs_1_.refs_2_
  113.1 10.8 attend.5
  124.0 11.0 attend.6
  141.2 5.9 project.4
  148.0 5.8 project.5
  155.1 5.9 project.6
  172.6 10.8 attend.7
  183.4 6.2 project.7
  189.6 12.1 collective-permute-done.28.refs_10_
  202.7 7.3 collective-permute-done.29.refs_11_
  210.4 14.6 %collective-permute-start.34 = (bf16[256,2176]{1,0:T(8,128)(2,1)S(1)}, bf16[256,2176]{1,0:T(8,128)(2,1)S(1)}, u32[]{:S(2)}, u32[]{:S(2)}) collective-permute-start(bf16[256,2176]{1,0:T(8,128)(2,1)S(1)} %copy-done.46), channel_id=1, source_target_pairs={{0,2},{1,3},{2,4},{3,5},{4,6},{5,7},{6,0},{7,1},{8,10},{9,11},{10,... | collective-permute-start | bytes 3342344 | tf_op jit(solution)/shard_map/ppermute | solution.py:706
  239.1 9.0 collective-permute-done.33.refs_15_
  248.8 48.0 %collective-permute-done.35.refs_17_ = bf16[256,2176]{1,0:T(8,128)(2,1)S(1)} collective-permute-done((bf16[256,2176]{1,0:T(8,128)(2,1)S(1)}, bf16[256,2176]{1,0:T(8,128)(2,1)S(1)}, u32[]{:S(2)}, u32[]{:S(2)}) %collective-permute-start.35) | collective-permute-done | bytes 1114144 | tf_op jit(solution)/shard_map/ppermute | solution.py:706
  296.8 23.9 %collective-permute-done.36.refs_18_ = bf16[256,2176]{1,0:T(8,128)(2,1)S(1)} collective-permute-done((bf16[256,2176]{1,0:T(8,128)(2,1)S(1)}, bf16[256,2176]{1,0:T(8,128)(2,1)S(1)}, u32[]{:S(2)}, u32[]{:S(2)}) %collective-permute-start.36) | collective-permute-done | bytes 1114144 | tf_op jit(solution)/shard_map/ppermute | solution.py:706
  321.7 398.8 %run_experts.1 = (f32[256,2176]{1,0:T(8,128)}, bf16[4,640,2048]{2,1,0:T(8,128)(2,1)}, bf16[4,256,2048]{2,1,0:T(8,128)(2,1)}, bf16[4,640,2048]{2,1,0:T(8,128)(2,1...) custom-call(s32[1]{0:T(128)} %bitcast.44.refs_0_, ...), custom_call_target="tpu_custom_call" | custom-call | flops 48318382080 | bytes 600000000 | tf_op jit(solution)/shard_map/run_experts/pallas_call | solution.py:421
  730.6 4.6 collective-permute-start.38
  735.9 12.7 %convolution_bitcast_fusion.1 = f32[1,2048,768]{2,1,0:T(8,128)} fusion(bf16[2560,2048]{1,0:T(8,128)(2,1)S(1)} %bitcast.287, bf16[2560,768]{1,0:T(8,128)(2,1)} %bitcast.291), kind=kOutput, calls=%fused_computation.24 | convolution fusion | flops 8053063680 | bytes 20709376 | tf_op jit(solution)/shard_map/dot_general | solution.py:39
  748.6 13.1 %convolution_bitcast_fusion.2 = f32[1,2048,768]{2,1,0:T(8,128)} fusion(bf16[2560,2048]{1,0:T(8,128)(2,1)S(1)} %bitcast.288, bf16[2560,768]{1,0:T(8,128)(2,1)} %bitcast.290), kind=kOutput, calls=%fused_computation.25 | convolution fusion | flops 8053063680 | bytes 20709376 | tf_op jit(solution)/shard_map/dot_general | solution.py:39
  763.8 10.7 convolution_bitcast_fusion
  775.8 14.4 %attend_back.4 = (bf16[256,1280]{1,0:T(8,128)(2,1)}, f32[256,2048]{1,0:T(8,128)}, f32[1,2048]{1,0:T(1,128)}, f32[1,128]{1,0:T(1,128)}, f32[1,128]{1,0:T(1,128)}) custom-call(s32[8]{0:T(128)} %stack.107.refs_0_, bf16[256,2048]{1,0:T(8,128)(2,1)} %copy-done.28, bf16[256,2048]{1,0:T(8,128)(2,1)} %refs_2_.5, s32[1,256]{1,0:T(1,128)} %refs_3_.3, ...), custom_call_target="tpu_custom_call" | custom-call | flops 3355443200 | bytes 23068672 | tf_op jit(solution)/shard_map/attend_back/pallas_call | solution.py:657
  790.2 4.5 slice_bitcast_fusion.1
  797.8 6.9 fusion
  824.6 13.9 %attend_back.5 = (bf16[256,1280]{1,0:T(8,128)(2,1)}, bf16[256,2048]{1,0:T(8,128)(2,1)}, f32[1,2048]{1,0:T(1,128)}, f32[1,128]{1,0:T(1,128)}, f32[1,128]{1,0:T(1,128)}) custom-call(s32[8]{0:T(128)} %stack.107.refs_0_, bf16[256,2048]{1,0:T(8,128)(2,1)} %collective-permute-done.37.refs_1_, bf16[256,2048]{1,0:T(8,128)(2,1)} %collective-permute-done.refs_1_.refs_2_, ...), custom_call_target="tpu_custom_call" | custom-call | flops 3355443200 | bytes 23068672 | tf_op jit(solution)/shard_map/attend_back/pallas_call | solution.py:657
  842.5 14.1 %attend_back.6 = (bf16[256,1280]{1,0:T(8,128)(2,1)}, bf16[256,2048]{1,0:T(8,128)(2,1)}, f32[1,2048]{1,0:T(1,128)}, f32[1,128]{1,0:T(1,128)}, f32[1,128]{1,0:T(1,128)}) custom-call(s32[8]{0:T(128)} %stack.107.refs_0_, bf16[256,2048]{1,0:T(8,128)(2,1)} %collective-permute-done.38.refs_1_, bf16[256,2048]{1,0:T(8,128)(2,1)} %collective-permute-done.14.refs_1_.refs_2_, ...), custom_call_target="tpu_custom_call" | custom-call | flops 3355443200 | bytes 23068672 | tf_op jit(solution)/shard_map/attend_back/pallas_call | solution.py:657
  869.7 4.6 collective-permute-done.43.refs_3_
  874.3 13.5 %collective-permute-done.42.refs_2_ = bf16[160,2048]{1,0:T(8,128)(2,1)} collective-permute-done((bf16[160,2048]{1,0:T(8,128)(2,1)}, bf16[160,2048]{1,0:T(8,128)(2,1)}, u32[]{:S(2)}, u32[]{:S(2)}) %collective-permute-start.42) | collective-permute-done | bytes 655392 | tf_op jit(solution)/shard_map/ppermute | solution.py:701
  887.8 7.6 combine_slots.5
  895.4 7.5 combine_slots.4
  902.9 14.0 %attend_back.7 = (bf16[256,1280]{1,0:T(8,128)(2,1)}, bf16[256,2048]{1,0:T(8,128)(2,1)}, f32[1,2048]{1,0:T(1,128)}, f32[1,128]{1,0:T(1,128)}, f32[1,128]{1,0:T(1,128)}) custom-call(s32[8]{0:T(128)} %stack.107.refs_0_, bf16[256,2048]{1,0:T(8,128)(2,1)} %collective-permute-done.39.refs_1_, bf16[256,2048]{1,0:T(8,128)(2,1)} %collective-permute-done.13.refs_1_.refs_2_, ...), custom_call_target="tpu_custom_call" | custom-call | flops 3355443200 | bytes 23068672 | tf_op jit(solution)/shard_map/attend_back/pallas_call | solution.py:657
  917.0 8.8 fusion.8
  947.0 13.9 %collective-permute-done.59 = bf16[256,2048]{1,0:T(8,128)(2,1)S(1)} collective-permute-done((bf16[256,2048]{1,0:T(8,128)(2,1)}, bf16[256,2048]{1,0:T(8,128)(2,1)S(1)}, u32[]{:S(2)}, u32[]{:S(2)}) %collective-permute-start.59) | collective-permute-done | bytes 1048608 | tf_op jit(solution)/shard_map/ppermute | solution.py:701
  963.8 21.0 %collective-permute-done.61 = bf16[256,2048]{1,0:T(8,128)(2,1)S(1)} collective-permute-done((bf16[256,2048]{1,0:T(8,128)(2,1)}, bf16[256,2048]{1,0:T(8,128)(2,1)S(1)}, u32[]{:S(2)}, u32[]{:S(2)}) %collective-permute-start.61) | collective-permute-done | bytes 1048608 | tf_op jit(solution)/shard_map/ppermute | solution.py:701
  988.0 11.5 collective-permute-done.57.refs_7_
  999.5 13.3 %collective-permute-done.56.refs_6_ = bf16[160,2048]{1,0:T(8,128)(2,1)S(1)} collective-permute-done((bf16[160,2048]{1,0:T(8,128)(2,1)S(1)}, bf16[160,2048]{1,0:T(8,128)(2,1)S(1)}, u32[]{:S(2)}, u32[]{:S(2)}) %collective-permute-start.56) | collective-permute-done | bytes 655392 | tf_op jit(solution)/shard_map/ppermute | solution.py:701
  1029.2 12.2 %collective-permute-done.54.refs_4_ = bf16[160,2048]{1,0:T(8,128)(2,1)} collective-permute-done((bf16[160,2048]{1,0:T(8,128)(2,1)S(1)}, bf16[160,2048]{1,0:T(8,128)(2,1)}, u32[]{:S(2)}, u32[]{:S(2)}) %collective-permute-start.54) | collective-permute-done | bytes 655392 | tf_op jit(solution)/shard_map/ppermute | solution.py:701
  1046.5 7.7 combine_slots.7
  1054.3 9.6 collective-permute-done.64
  1070.8 5.4 fusion.32
  1078.5 7.5 combine_slots.6
  1093.9 8.7 collective-permute-done.70
  1102.6 36.5 %collective-permute-done.71 = bf16[256,1280]{1,0:T(8,128)(2,1)} collective-permute-done((bf16[256,1280]{1,0:T(8,128)(2,1)}, bf16[256,1280]{1,0:T(8,128)(2,1)}, u32[]{:S(2)}, u32[]{:S(2)}) %collective-permute-start.71) | collective-permute-done | bytes 655392 | tf_op jit(solution)/shard_map/ppermute | solution.py:706
  1143.1 40.9 %collective-permute-done.49 = bf16[256,2048]{1,0:T(8,128)(2,1)} collective-permute-done((bf16[256,2048]{1,0:T(8,128)(2,1)}, bf16[256,2048]{1,0:T(8,128)(2,1)}, u32[]{:S(2)}, u32[]{:S(2)}) %collective-permute-start.49) | collective-permute-done | bytes 1048608 | tf_op jit(solution)/shard_map/ppermute | solution.py:706
  1184.0 22.4 %collective-permute-done.48 = bf16[256,2048]{1,0:T(8,128)(2,1)} collective-permute-done((bf16[256,2048]{1,0:T(8,128)(2,1)S(1)}, bf16[256,2048]{1,0:T(8,128)(2,1)}, u32[]{:S(2)}, u32[]{:S(2)}) %collective-permute-start.48) | collective-permute-done | bytes 1048608 | tf_op jit(solution)/shard_map/ppermute | solution.py:706
  1206.4 5.5 collective-permute-done.58
  (466 shorter events, 233.2 us)
Async XLA Ops:
  8.7 27.7 %collective-permute-start.9 = (bf16[256,1280]{1,0:T(8,128)(2,1)S(1)}, bf16[256,1280]{1,0:T(8,128)(2,1)S(1)}, u32[]{:S(2)}, u32[]{:S(2)}) collective-permute-start(bf16[256,1280]{1,0:T(8,128)(2,1)S(1)} %pad_maximum_fusion.1.refs_9_.refs_22_), channel_id=1, source_target_pairs={{0,4},{1,5},{2,6},{3,7},{4,0},{5,1},{6,2},{7,3},{8,12},{9,13},{10,... | collective-permute-start | bytes 1966088 | tf_op jit(solution)/shard_map/ppermute | solution.py:706
  9.3 57.0 %collective-permute-start.11 = (bf16[256,1280]{1,0:T(8,128)(2,1)S(1)}, bf16[256,1280]{1,0:T(8,128)(2,1)S(1)}, u32[]{:S(2)}, u32[]{:S(2)}) collective-permute-start(bf16[256,1280]{1,0:T(8,128)(2,1)S(1)} %pad_maximum_fusion.1.refs_9_.refs_22_), channel_id=1, source_target_pairs={{0,6},{1,7},{2,0},{3,1},{4,2},{5,3},{6,4},{7,5},{8,14},{9,15},{10,... | collective-permute-start | bytes 1966088 | tf_op jit(solution)/shard_map/ppermute | solution.py:706
  16.2 52.5 %collective-permute-start.7 = (bf16[256,1280]{1,0:T(8,128)(2,1)S(1)}, bf16[256,1280]{1,0:T(8,128)(2,1)S(1)}, u32[]{:S(2)}, u32[]{:S(2)}) collective-permute-start(bf16[256,1280]{1,0:T(8,128)(2,1)S(1)} %pad_maximum_fusion.1.refs_9_.refs_22_), channel_id=1, source_target_pairs={{0,2},{1,3},{2,4},{3,5},{4,6},{5,7},{6,0},{7,1},{8,10},{9,11},{10,... | collective-permute-start | bytes 1966088 | tf_op jit(solution)/shard_map/ppermute | solution.py:706
  36.4 33.4 %collective-permute-start.6 = (bf16[256,1280]{1,0:T(8,128)(2,1)S(1)}, bf16[256,1280]{1,0:T(8,128)(2,1)S(1)}, u32[]{:S(2)}, u32[]{:S(2)}) collective-permute-start(bf16[256,1280]{1,0:T(8,128)(2,1)S(1)} %pad_maximum_fusion.1.refs_9_.refs_22_), channel_id=1, source_target_pairs={{0,1},{1,0},{2,3},{3,2},{4,5},{5,4},{6,7},{7,6},{8,9},{9,8},{10,11... | collective-permute-start | bytes 1966088 | tf_op jit(solution)/shard_map/ppermute | solution.py:701
  41.7 28.8 %collective-permute-start.10 = (bf16[256,1280]{1,0:T(8,128)(2,1)S(1)}, bf16[256,1280]{1,0:T(8,128)(2,1)}, u32[]{:S(2)}, u32[]{:S(2)}) collective-permute-start(bf16[256,1280]{1,0:T(8,128)(2,1)S(1)} %collective-permute-done.9.refs_13_.refs_26_), channel_id=1, source_target_pairs={{0,1},{1,0},{2,3},{3,2},{4,5},{5,4},{6,7},{7,6},{8,9},{9,8},{10,11... | collective-permute-start | bytes 1966088 | tf_op jit(solution)/shard_map/ppermute | solution.py:701
  55.3 35.2 %collective-permute-start = (bf16[256,2048]{1,0:T(8,128)(2,1)}, bf16[256,2048]{1,0:T(8,128)(2,1)}, u32[]{:S(2)}, u32[]{:S(2)}) collective-permute-start(bf16[256,2048]{1,0:T(8,128)(2,1)} %refs_2_.5), channel_id=1, source_target_pairs={{0,8},{1,9},{2,10},{3,11},{4,12},{5,13},{6,14},{7,15},{8,0},{9,1},... | collective-permute-start | bytes 3145736 | tf_op jit(solution)/shard_map/ppermute | solution.py:701
  66.3 46.9 %collective-permute-start.14 = (bf16[256,2048]{1,0:T(8,128)(2,1)}, bf16[256,2048]{1,0:T(8,128)(2,1)}, u32[]{:S(2)}, u32[]{:S(2)}) collective-permute-start(bf16[256,2048]{1,0:T(8,128)(2,1)} %refs_2_.5), channel_id=1, source_target_pairs={{0,16},{1,17},{2,18},{3,19},{4,20},{5,21},{6,22},{7,23},{8,24},{9,... | collective-permute-start | bytes 3145736 | tf_op jit(solution)/shard_map/ppermute | solution.py:701
  68.6 55.3 %collective-permute-start.13 = (bf16[256,2048]{1,0:T(8,128)(2,1)}, bf16[256,2048]{1,0:T(8,128)(2,1)}, u32[]{:S(2)}, u32[]{:S(2)}) collective-permute-start(bf16[256,2048]{1,0:T(8,128)(2,1)} %refs_2_.5), channel_id=1, source_target_pairs={{0,24},{1,25},{2,26},{3,27},{4,28},{5,29},{6,30},{7,31},{8,16},{9,... | collective-permute-start | bytes 3145736 | tf_op jit(solution)/shard_map/ppermute | solution.py:701
  74.4 62.2 %collective-permute-start.22 = (bf16[128,2048]{1,0:T(8,128)(2,1)}, bf16[128,2048]{1,0:T(8,128)(2,1)}, u32[]{:S(2)}, u32[]{:S(2)}) collective-permute-start(bf16[128,2048]{1,0:T(8,128)(2,1)} %refs_14_.3), channel_id=1, source_target_pairs={{0,6},{1,7},{2,0},{3,1},{4,2},{5,3},{6,4},{7,5},{8,14},{9,15},{10,... | collective-permute-start | bytes 1572872 | tf_op jit(solution)/shard_map/ppermute | solution.py:706
  86.6 50.1 %collective-permute-start.20 = (bf16[128,2048]{1,0:T(8,128)(2,1)}, bf16[128,2048]{1,0:T(8,128)(2,1)}, u32[]{:S(2)}, u32[]{:S(2)}) collective-permute-start(bf16[128,2048]{1,0:T(8,128)(2,1)} %refs_14_.3), channel_id=1, source_target_pairs={{0,4},{1,5},{2,6},{3,7},{4,0},{5,1},{6,2},{7,3},{8,12},{9,13},{10,... | collective-permute-start | bytes 1572872 | tf_op jit(solution)/shard_map/ppermute | solution.py:706
  90.6 46.6 %collective-permute-start.18 = (bf16[128,2048]{1,0:T(8,128)(2,1)}, bf16[128,2048]{1,0:T(8,128)(2,1)}, u32[]{:S(2)}, u32[]{:S(2)}) collective-permute-start(bf16[128,2048]{1,0:T(8,128)(2,1)} %refs_14_.3), channel_id=1, source_target_pairs={{0,2},{1,3},{2,4},{3,5},{4,6},{5,7},{6,0},{7,1},{8,10},{9,11},{10,... | collective-permute-start | bytes 1572872 | tf_op jit(solution)/shard_map/ppermute | solution.py:706
  147.1 63.3 %collective-permute-start.24 = (bf16[256,2048]{1,0:T(8,128)(2,1)}, bf16[256,2048]{1,0:T(8,128)(2,1)}, u32[]{:S(2)}, u32[]{:S(2)}) collective-permute-start(bf16[256,2048]{1,0:T(8,128)(2,1)} %project.4), channel_id=1, source_target_pairs={{0,8},{1,9},{2,10},{3,11},{4,12},{5,13},{6,14},{7,15},{8,0},{9,1},... | collective-permute-start | bytes 3145736 | tf_op jit(solution)/shard_map/ppermute | solution.py:701
  153.8 71.2 %collective-permute-start.25 = (bf16[256,2048]{1,0:T(8,128)(2,1)}, bf16[256,2048]{1,0:T(8,128)(2,1)}, u32[]{:S(2)}, u32[]{:S(2)}) collective-permute-start(bf16[256,2048]{1,0:T(8,128)(2,1)} %project.5), channel_id=1, source_target_pairs={{0,16},{1,17},{2,18},{3,19},{4,20},{5,21},{6,22},{7,23},{8,24},{9,... | collective-permute-start | bytes 3145736 | tf_op jit(solution)/shard_map/ppermute | solution.py:701
  160.9 64.1 %collective-permute-start.26 = (bf16[256,2048]{1,0:T(8,128)(2,1)}, bf16[256,2048]{1,0:T(8,128)(2,1)}, u32[]{:S(2)}, u32[]{:S(2)}) collective-permute-start(bf16[256,2048]{1,0:T(8,128)(2,1)} %project.6), channel_id=1, source_target_pairs={{0,24},{1,25},{2,26},{3,27},{4,28},{5,29},{6,30},{7,31},{8,16},{9,... | collective-permute-start | bytes 3145736 | tf_op jit(solution)/shard_map/ppermute | solution.py:701
  169.4 32.4 %collective-permute-start.28 = (bf16[80,2176]{1,0:T(8,128)(2,1)}, bf16[80,2176]{1,0:T(8,128)(2,1)S(1)}, u32[]{:S(2)}, u32[]{:S(2)}) collective-permute-start(bf16[80,2176]{1,0:T(8,128)(2,1)} %get-tuple-element.124), channel_id=1, source_target_pairs={{0,8},{1,9},{2,10},{3,11},{4,12},{5,13},{6,14},{7,15},{8,0},{9,1},... | collective-permute-start | bytes 1044488 | tf_op jit(solution)/shard_map/ppermute | solution.py:701
  170.3 39.7 %collective-permute-start.29 = (bf16[80,2176]{1,0:T(8,128)(2,1)}, bf16[80,2176]{1,0:T(8,128)(2,1)}, u32[]{:S(2)}, u32[]{:S(2)}) collective-permute-start(bf16[80,2176]{1,0:T(8,128)(2,1)} %get-tuple-element.125), channel_id=1, source_target_pairs={{0,9},{1,8},{2,11},{3,10},{4,13},{5,12},{6,15},{7,14},{8,1},{9,0},... | collective-permute-start | bytes 1044488 | tf_op jit(solution)/shard_map/ppermute | solution.py:701
  201.8 28.0 %collective-permute-start.30 = (bf16[80,2176]{1,0:T(8,128)(2,1)}, bf16[80,2176]{1,0:T(8,128)(2,1)S(1)}, u32[]{:S(2)}, u32[]{:S(2)}) collective-permute-start(bf16[80,2176]{1,0:T(8,128)(2,1)} %get-tuple-element.126), channel_id=1, source_target_pairs={{0,16},{1,17},{2,18},{3,19},{4,20},{5,21},{6,22},{7,23},{8,24},{9,... | collective-permute-start | bytes 1044488 | tf_op jit(solution)/shard_map/ppermute | solution.py:701
  210.4 38.4 %collective-permute-start.34 = (bf16[256,2176]{1,0:T(8,128)(2,1)S(1)}, bf16[256,2176]{1,0:T(8,128)(2,1)S(1)}, u32[]{:S(2)}, u32[]{:S(2)}) collective-permute-start(bf16[256,2176]{1,0:T(8,128)(2,1)S(1)} %copy-done.46), channel_id=1, source_target_pairs={{0,2},{1,3},{2,4},{3,5},{4,6},{5,7},{6,0},{7,1},{8,10},{9,11},{10,... | collective-permute-start | bytes 3342344 | tf_op jit(solution)/shard_map/ppermute | solution.py:706
  225.1 71.8 %collective-permute-start.35 = (bf16[256,2176]{1,0:T(8,128)(2,1)S(1)}, bf16[256,2176]{1,0:T(8,128)(2,1)S(1)}, u32[]{:S(2)}, u32[]{:S(2)}) collective-permute-start(bf16[256,2176]{1,0:T(8,128)(2,1)S(1)} %copy-done.46), channel_id=1, source_target_pairs={{0,4},{1,5},{2,6},{3,7},{4,0},{5,1},{6,2},{7,3},{8,12},{9,13},{10,... | collective-permute-start | bytes 3342344 | tf_op jit(solution)/shard_map/ppermute | solution.py:706
  225.1 95.7 %collective-permute-start.36 = (bf16[256,2176]{1,0:T(8,128)(2,1)S(1)}, bf16[256,2176]{1,0:T(8,128)(2,1)S(1)}, u32[]{:S(2)}, u32[]{:S(2)}) collective-permute-start(bf16[256,2176]{1,0:T(8,128)(2,1)S(1)} %copy-done.46), channel_id=1, source_target_pairs={{0,6},{1,7},{2,0},{3,1},{4,2},{5,3},{6,4},{7,5},{8,14},{9,15},{10,... | collective-permute-start | bytes 3342344 | tf_op jit(solution)/shard_map/ppermute | solution.py:706
  730.3 59.9 %collective-permute-start.37 = (bf16[256,2048]{1,0:T(8,128)(2,1)S(1)}, bf16[256,2048]{1,0:T(8,128)(2,1)}, u32[]{:S(2)}, u32[]{:S(2)}) collective-permute-start(bf16[256,2048]{1,0:T(8,128)(2,1)S(1)} %get-tuple-element.262.refs_1_), channel_id=1, source_target_pairs={{0,8},{1,9},{2,10},{3,11},{4,12},{5,13},{6,14},{7,15},{8,0},{9,1},... | collective-permute-start | bytes 3145736 | tf_op jit(solution)/shard_map/ppermute | solution.py:701
  730.6 59.6 %collective-permute-start.38 = (bf16[256,2048]{1,0:T(8,128)(2,1)S(1)}, bf16[256,2048]{1,0:T(8,128)(2,1)}, u32[]{:S(2)}, u32[]{:S(2)}) collective-permute-start(bf16[256,2048]{1,0:T(8,128)(2,1)S(1)} %get-tuple-element.262.refs_1_), channel_id=1, source_target_pairs={{0,16},{1,17},{2,18},{3,19},{4,20},{5,21},{6,22},{7,23},{8,24},{9,... | collective-permute-start | bytes 3145736 | tf_op jit(solution)/shard_map/ppermute | solution.py:701
  735.2 55.0 %collective-permute-start.39 = (bf16[256,2048]{1,0:T(8,128)(2,1)S(1)}, bf16[256,2048]{1,0:T(8,128)(2,1)}, u32[]{:S(2)}, u32[]{:S(2)}) collective-permute-start(bf16[256,2048]{1,0:T(8,128)(2,1)S(1)} %get-tuple-element.262.refs_1_), channel_id=1, source_target_pairs={{0,24},{1,25},{2,26},{3,27},{4,28},{5,29},{6,30},{7,31},{8,16},{9,... | collective-permute-start | bytes 3145736 | tf_op jit(solution)/shard_map/ppermute | solution.py:701
  806.6 51.9 %collective-permute-start.40 = (bf16[4,128,2048]{2,1,0:T(8,128)(2,1)}, bf16[4,128,2048]{2,1,0:T(8,128)(2,1)}, u32[]{:S(2)}, u32[]{:S(2)}) collective-permute-start(bf16[4,128,2048]{2,1,0:T(8,128)(2,1)} %fusion.34), channel_id=1, source_target_pairs={{0,1},{1,0},{2,3},{3,2},{4,5},{5,4},{6,7},{7,6},{8,9},{9,8},{10,11... | collective-permute-start | bytes 6291464 | tf_op jit(solution)/shard_map/ppermute | solution.py:701
  809.3 47.3 %collective-permute-start.47 = (bf16[160,2048]{1,0:T(8,128)(2,1)}, bf16[160,2048]{1,0:T(8,128)(2,1)S(1)}, u32[]{:S(2)}, u32[]{:S(2)}) collective-permute-start(bf16[160,2048]{1,0:T(8,128)(2,1)} %pad_maximum_fusion.9), channel_id=1, source_target_pairs={{0,25},{1,24},{2,27},{3,26},{4,29},{5,28},{6,31},{7,30},{8,17},{9,... | collective-permute-start | bytes 1966088 | tf_op jit(solution)/shard_map/ppermute | solution.py:701
  812.1 45.3 %collective-permute-start.46 = (bf16[160,2048]{1,0:T(8,128)(2,1)}, bf16[160,2048]{1,0:T(8,128)(2,1)S(1)}, u32[]{:S(2)}, u32[]{:S(2)}) collective-permute-start(bf16[160,2048]{1,0:T(8,128)(2,1)} %pad_maximum_fusion.8), channel_id=1, source_target_pairs={{0,24},{1,25},{2,26},{3,27},{4,28},{5,29},{6,30},{7,31},{8,16},{9,... | collective-permute-start | bytes 1966088 | tf_op jit(solution)/shard_map/ppermute | solution.py:701
  813.8 52.6 %collective-permute-start.45 = (bf16[160,2048]{1,0:T(8,128)(2,1)}, bf16[160,2048]{1,0:T(8,128)(2,1)}, u32[]{:S(2)}, u32[]{:S(2)}) collective-permute-start(bf16[160,2048]{1,0:T(8,128)(2,1)} %pad_maximum_fusion.7), channel_id=1, source_target_pairs={{0,17},{1,16},{2,19},{3,18},{4,21},{5,20},{6,23},{7,22},{8,25},{9,... | collective-permute-start | bytes 1966088 | tf_op jit(solution)/shard_map/ppermute | solution.py:701
  816.7 53.1 %collective-permute-start.44 = (bf16[160,2048]{1,0:T(8,128)(2,1)}, bf16[160,2048]{1,0:T(8,128)(2,1)}, u32[]{:S(2)}, u32[]{:S(2)}) collective-permute-start(bf16[160,2048]{1,0:T(8,128)(2,1)} %pad_maximum_fusion.6), channel_id=1, source_target_pairs={{0,16},{1,17},{2,18},{3,19},{4,20},{5,21},{6,22},{7,23},{8,24},{9,... | collective-permute-start | bytes 1966088 | tf_op jit(solution)/shard_map/ppermute | solution.py:701
  857.4 30.4 %collective-permute-start.42 = (bf16[160,2048]{1,0:T(8,128)(2,1)}, bf16[160,2048]{1,0:T(8,128)(2,1)}, u32[]{:S(2)}, u32[]{:S(2)}) collective-permute-start(bf16[160,2048]{1,0:T(8,128)(2,1)} %pad_maximum_fusion.4), channel_id=1, source_target_pairs={{0,8},{1,9},{2,10},{3,11},{4,12},{5,13},{6,14},{7,15},{8,0},{9,1},... | collective-permute-start | bytes 1966088 | tf_op jit(solution)/shard_map/ppermute | solution.py:701
  858.5 29.3 %collective-permute-start.41 = (bf16[160,2048]{1,0:T(8,128)(2,1)}, bf16[160,2048]{1,0:T(8,128)(2,1)}, u32[]{:S(2)}, u32[]{:S(2)}) collective-permute-start(bf16[160,2048]{1,0:T(8,128)(2,1)} %pad_maximum_fusion.3), channel_id=1, source_target_pairs={{0,1},{1,0},{2,3},{3,2},{4,5},{5,4},{6,7},{7,6},{8,9},{9,8},{10,11... | collective-permute-start | bytes 1966088 | tf_op jit(solution)/shard_map/ppermute | solution.py:701
  866.4 78.2 %collective-permute-start.60 = (bf16[256,2048]{1,0:T(8,128)(2,1)}, bf16[256,2048]{1,0:T(8,128)(2,1)}, u32[]{:S(2)}, u32[]{:S(2)}) collective-permute-start(bf16[256,2048]{1,0:T(8,128)(2,1)} %get-tuple-element.166), channel_id=1, source_target_pairs={{0,16},{1,17},{2,18},{3,19},{4,20},{5,21},{6,22},{7,23},{8,24},{9,... | collective-permute-start | bytes 3145736 | tf_op jit(solution)/shard_map/ppermute | solution.py:701
  869.7 66.2 %collective-permute-start.72 = (bf16[128,2048]{1,0:T(8,128)(2,1)}, bf16[128,2048]{1,0:T(8,128)(2,1)}, u32[]{:S(2)}, u32[]{:S(2)}) collective-permute-start(bf16[128,2048]{1,0:T(8,128)(2,1)} %get-tuple-element.305), channel_id=1, source_target_pairs={{0,2},{1,3},{2,4},{3,5},{4,6},{5,7},{6,0},{7,1},{8,10},{9,11},{10,... | collective-permute-start | bytes 1572872 | tf_op jit(solution)/shard_map/ppermute | solution.py:706
  874.3 62.1 %collective-permute-start.73 = (bf16[128,2048]{1,0:T(8,128)(2,1)}, bf16[128,2048]{1,0:T(8,128)(2,1)}, u32[]{:S(2)}, u32[]{:S(2)}) collective-permute-start(bf16[128,2048]{1,0:T(8,128)(2,1)} %get-tuple-element.304), channel_id=1, source_target_pairs={{0,4},{1,5},{2,6},{3,7},{4,0},{5,1},{6,2},{7,3},{8,12},{9,13},{10,... | collective-permute-start | bytes 1572872 | tf_op jit(solution)/shard_map/ppermute | solution.py:706
  887.8 51.0 %collective-permute-start.74 = (bf16[128,2048]{1,0:T(8,128)(2,1)}, bf16[128,2048]{1,0:T(8,128)(2,1)}, u32[]{:S(2)}, u32[]{:S(2)}) collective-permute-start(bf16[128,2048]{1,0:T(8,128)(2,1)} %get-tuple-element.303), channel_id=1, source_target_pairs={{0,6},{1,7},{2,0},{3,1},{4,2},{5,3},{6,4},{7,5},{8,14},{9,15},{10,... | collective-permute-start | bytes 1572872 | tf_op jit(solution)/shard_map/ppermute | solution.py:706
  931.6 81.4 %collective-permute-start.50 = (bf16[4,256,1280]{2,1,0:T(8,128)(2,1)}, bf16[4,256,1280]{2,1,0:T(8,128)(2,1)}, u32[]{:S(2)}, u32[]{:S(2)}) collective-permute-start(bf16[4,256,1280]{2,1,0:T(8,128)(2,1)} %fusion.17), channel_id=1, source_target_pairs={{0,1},{1,0},{2,3},{3,2},{4,5},{5,4},{6,7},{7,6},{8,9},{9,8},{10,11... | collective-permute-start | bytes 7864328 | tf_op jit(solution)/shard_map/ppermute | solution.py:701
  936.4 48.3 %collective-permute-start.61 = (bf16[256,2048]{1,0:T(8,128)(2,1)}, bf16[256,2048]{1,0:T(8,128)(2,1)S(1)}, u32[]{:S(2)}, u32[]{:S(2)}) collective-permute-start(bf16[256,2048]{1,0:T(8,128)(2,1)} %get-tuple-element.167), channel_id=1, source_target_pairs={{0,24},{1,25},{2,26},{3,27},{4,28},{5,29},{6,30},{7,31},{8,16},{9,... | collective-permute-start | bytes 3145736 | tf_op jit(solution)/shard_map/ppermute | solution.py:701
  944.6 54.9 %collective-permute-start.57 = (bf16[160,2048]{1,0:T(8,128)(2,1)S(1)}, bf16[160,2048]{1,0:T(8,128)(2,1)S(1)}, u32[]{:S(2)}, u32[]{:S(2)}) collective-permute-start(bf16[160,2048]{1,0:T(8,128)(2,1)S(1)} %copy-done.53), channel_id=1, source_target_pairs={{0,25},{1,24},{2,27},{3,26},{4,29},{5,28},{6,31},{7,30},{8,17},{9,... | collective-permute-start | bytes 1966088 | tf_op jit(solution)/shard_map/ppermute | solution.py:701
  944.7 68.2 %collective-permute-start.56 = (bf16[160,2048]{1,0:T(8,128)(2,1)S(1)}, bf16[160,2048]{1,0:T(8,128)(2,1)S(1)}, u32[]{:S(2)}, u32[]{:S(2)}) collective-permute-start(bf16[160,2048]{1,0:T(8,128)(2,1)S(1)} %copy-done.52), channel_id=1, source_target_pairs={{0,24},{1,25},{2,26},{3,27},{4,28},{5,29},{6,30},{7,31},{8,16},{9,... | collective-permute-start | bytes 1966088 | tf_op jit(solution)/shard_map/ppermute | solution.py:701
  960.9 66.5 %collective-permute-start.55 = (bf16[160,2048]{1,0:T(8,128)(2,1)S(1)}, bf16[160,2048]{1,0:T(8,128)(2,1)}, u32[]{:S(2)}, u32[]{:S(2)}) collective-permute-start(bf16[160,2048]{1,0:T(8,128)(2,1)S(1)} %copy-done.51), channel_id=1, source_target_pairs={{0,17},{1,16},{2,19},{3,18},{4,21},{5,20},{6,23},{7,22},{8,25},{9,... | collective-permute-start | bytes 1966088 | tf_op jit(solution)/shard_map/ppermute | solution.py:701
  984.7 56.7 %collective-permute-start.54 = (bf16[160,2048]{1,0:T(8,128)(2,1)S(1)}, bf16[160,2048]{1,0:T(8,128)(2,1)}, u32[]{:S(2)}, u32[]{:S(2)}) collective-permute-start(bf16[160,2048]{1,0:T(8,128)(2,1)S(1)} %copy-done.50), channel_id=1, source_target_pairs={{0,16},{1,17},{2,18},{3,19},{4,20},{5,21},{6,22},{7,23},{8,24},{9,... | collective-permute-start | bytes 1966088 | tf_op jit(solution)/shard_map/ppermute | solution.py:701
  999.5 41.9 %collective-permute-start.53 = (bf16[160,2048]{1,0:T(8,128)(2,1)S(1)}, bf16[160,2048]{1,0:T(8,128)(2,1)}, u32[]{:S(2)}, u32[]{:S(2)}) collective-permute-start(bf16[160,2048]{1,0:T(8,128)(2,1)S(1)} %copy-done.49), channel_id=1, source_target_pairs={{0,9},{1,8},{2,11},{3,10},{4,13},{5,12},{6,15},{7,14},{8,1},{9,0},... | collective-permute-start | bytes 1966088 | tf_op jit(solution)/shard_map/ppermute | solution.py:701
  1012.8 33.1 %collective-permute-start.52 = (bf16[160,2048]{1,0:T(8,128)(2,1)}, bf16[160,2048]{1,0:T(8,128)(2,1)}, u32[]{:S(2)}, u32[]{:S(2)}) collective-permute-start(bf16[160,2048]{1,0:T(8,128)(2,1)} %pad_maximum_fusion.12), channel_id=1, source_target_pairs={{0,8},{1,9},{2,10},{3,11},{4,12},{5,13},{6,14},{7,15},{8,0},{9,1},... | collective-permute-start | bytes 1966088 | tf_op jit(solution)/shard_map/ppermute | solution.py:701
  1013.7 32.9 %collective-permute-start.51 = (bf16[160,2048]{1,0:T(8,128)(2,1)}, bf16[160,2048]{1,0:T(8,128)(2,1)}, u32[]{:S(2)}, u32[]{:S(2)}) collective-permute-start(bf16[160,2048]{1,0:T(8,128)(2,1)} %pad_maximum_fusion.11), channel_id=1, source_target_pairs={{0,1},{1,0},{2,3},{3,2},{4,5},{5,4},{6,7},{7,6},{8,9},{9,8},{10,11... | collective-permute-start | bytes 1966088 | tf_op jit(solution)/shard_map/ppermute | solution.py:701
  1045.9 44.4 %collective-permute-start.69 = (bf16[256,1280]{1,0:T(8,128)(2,1)}, bf16[256,1280]{1,0:T(8,128)(2,1)}, u32[]{:S(2)}, u32[]{:S(2)}) collective-permute-start(bf16[256,1280]{1,0:T(8,128)(2,1)} %get-tuple-element.302), channel_id=1, source_target_pairs={{0,2},{1,3},{2,4},{3,5},{4,6},{5,7},{6,0},{7,1},{8,10},{9,11},{10,... | collective-permute-start | bytes 1966088 | tf_op jit(solution)/shard_map/ppermute | solution.py:706
  1076.5 62.6 %collective-permute-start.71 = (bf16[256,1280]{1,0:T(8,128)(2,1)}, bf16[256,1280]{1,0:T(8,128)(2,1)}, u32[]{:S(2)}, u32[]{:S(2)}) collective-permute-start(bf16[256,1280]{1,0:T(8,128)(2,1)} %get-tuple-element.300), channel_id=1, source_target_pairs={{0,6},{1,7},{2,0},{3,1},{4,2},{5,3},{6,4},{7,5},{8,14},{9,15},{10,... | collective-permute-start | bytes 1966088 | tf_op jit(solution)/shard_map/ppermute | solution.py:706
  1086.0 98.0 %collective-permute-start.49 = (bf16[256,2048]{1,0:T(8,128)(2,1)}, bf16[256,2048]{1,0:T(8,128)(2,1)}, u32[]{:S(2)}, u32[]{:S(2)}) collective-permute-start(bf16[256,2048]{1,0:T(8,128)(2,1)} %combine_slots.5), channel_id=1, source_target_pairs={{0,4},{1,5},{2,6},{3,7},{4,0},{5,1},{6,2},{7,3},{8,12},{9,13},{10,... | collective-permute-start | bytes 3145736 | tf_op jit(solution)/shard_map/ppermute | solution.py:706
  1089.3 117.1 %collective-permute-start.48 = (bf16[256,2048]{1,0:T(8,128)(2,1)S(1)}, bf16[256,2048]{1,0:T(8,128)(2,1)}, u32[]{:S(2)}, u32[]{:S(2)}) collective-permute-start(bf16[256,2048]{1,0:T(8,128)(2,1)S(1)} %copy-done.47), channel_id=1, source_target_pairs={{0,6},{1,7},{2,0},{3,1},{4,2},{5,3},{6,4},{7,5},{8,14},{9,15},{10,... | collective-permute-start | bytes 3145736 | tf_op jit(solution)/shard_map/ppermute | solution.py:706
  1090.4 121.6 %collective-permute-start.58 = (bf16[256,2048]{1,0:T(8,128)(2,1)}, bf16[256,2048]{1,0:T(8,128)(2,1)}, u32[]{:S(2)}, u32[]{:S(2)}) collective-permute-start(bf16[256,2048]{1,0:T(8,128)(2,1)} %combine_slots.6), channel_id=1, source_target_pairs={{0,2},{1,3},{2,4},{3,5},{4,6},{5,7},{6,0},{7,1},{8,10},{9,11},{10,... | collective-permute-start | bytes 3145736 | tf_op jit(solution)/shard_map/ppermute | solution.py:706
  (122 other events, 2473.3 us)
where the time goes:
time: 1220 us
  Pallas kernels  557 us (46%)
  waiting for transfers between devices  346 us (28%)
  starting transfers between devices  111 us (9%)
  other arithmetic  75.2 us (6%)
  local copies, waits for them, and re-layouts  67.9 us (6%)
  matrix products  56.7 us (5%)
    pallas_call x1, Pallas kernels, run_experts(): pl.pallas_call(lambda *refs: experts_kernel(nf, nz, cap, *refs), in_specs...  399 us
    ppermute x21, waiting for transfers between devices, along(): lax.ppermute(value, 'expert', [(j, (j + 2 * k) % ne) for j in range(ne)])  196 us
    ppermute x51, waiting for transfers between devices, across(): lax.ppermute(value, ALL, [(i * ne + j, (i ^ df) * ne + (j ^ dc)) for i in...  137 us
    pallas_call x4, Pallas kernels, attend_back(): pl.pallas_call(lambda *refs: attend_back_kernel(len(w_blocks), heads, kv_...  56.4 us
    ppermute x51, starting transfers between devices, across(): lax.ppermute(value, ALL, [(i * ne + j, (i ^ df) * ne + (j ^ dc)) for i in...  56.2 us
    dot_general x6, matrix products, left_product(): lax.dot_general(left, right, (((0,), (0,)), ((), ())), preferred_element_...  53.2 us
    ppermute x21, starting transfers between devices, along(): lax.ppermute(value, 'expert', [(j, (j + 2 * k) % ne) for j in range(ne)])  50.4 us
    pallas_call x4, Pallas kernels, attend(): pl.pallas_call(lambda *refs: attend_kernel(len(w_blocks), heads, kv_heads...  43.5 us
  transfers between devices with their start and end apart: 75, of which 29 were waited for; matrix products, arithmetic and copies ran while one was open for 13% of the time, Pallas kernels for 13%

commit v1 on v0

--- a/solution.py
+++ b/solution.py
@@ -744,16 +744,19 @@
             values = [a + b for a, b in zip(values[::2], values[1::2])]
         return values[0]
 
-    def sum_small(columns, row, *earlier):
-        blocks = columns.reshape(nz, 2, MODEL_WIDTH // ne, columns.shape[1])
-        rows = jnp.broadcast_to(row[None, None], (nz, 2) + row.shape)
-        blocks = jnp.concatenate([blocks, rows], axis=2)
+    def sum_small(lines, row):
+        own = MODEL_WIDTH // ne
+        blocks = jnp.transpose(lines.reshape(lines.shape[0], nz, 2, own), (1, 2, 0, 3))
+        rows = row.reshape(row.size // own, own)
+        rows = jnp.pad(rows, ((0, -(rows.shape[0] + lines.shape[0]) % 8), (0, 0)))
+        blocks = jnp.concatenate([blocks, jnp.broadcast_to(rows[None, None], (nz, 2) + rows.shape)], axis=2)
         mine = lax.dynamic_index_in_dim(blocks, c, 1, keepdims=False)
         mine = mine + across(lax.dynamic_index_in_dim(blocks, 1 - c, 1, keepdims=False), 0, 1)
-        mine = after(mine, *earlier)
-        sends = [lax.dynamic_index_in_dim(mine, z ^ step, 0, keepdims=False) for step in range(nz)]
-        pairs = [[(j, j ^ (2 * step)) for j in range(ne)] for step in range(nz)]
-        return add_pairs([lax.ppermute(v, "expert", p) if i else v for i, (v, p) in enumerate(zip(sends, pairs))])
+        got = [lax.dynamic_index_in_dim(mine, z, 0, keepdims=False)]
+        for step in range(1, nz):
+            part = lax.dynamic_index_in_dim(mine, z ^ step, 0, keepdims=False)
+            got.append(lax.ppermute(part, "expert", [(j, j ^ (2 * step)) for j in range(ne)]))
+        return add_pairs(got)
 
     width_q, width_k = w_query.shape[1], key_matrix.shape[1]
     w_heads = jnp.concatenate([w_query, key_matrix, value_matrix], axis=1)
@@ -858,7 +861,7 @@
     )
     d_logits = (gates * (d_gates - jnp.sum(gates * d_gates, axis=-1, keepdims=True))).astype(jnp.bfloat16)
 
-    router_grad = left_product(normed_two, d_logits)
+    router_grad = left_product(d_logits, normed_two)[:experts]
     d_normed_two = d_normed_two + right_product(d_logits, full_router[:, :experts])
     d_norm_part, gain_two_grad = row_norm_back(d_normed_two, residual_mid, rinv_two, gain_two)
     d_mid = cotangent.astype(jnp.float32) + d_norm_part
@@ -934,10 +937,8 @@
             gain_one_grad, q_gain_grad, k_gain_grad = sums
     normed_one = jnp.concatenate([attended[df][0] for df in range(nf)], axis=0)
     share_heads, head_parts = reduce_rows(left_product(normed_one, jnp.concatenate(d_heads, axis=0)))
-    columns = jnp.concatenate([router_grad, jnp.transpose(gain_one_grad), gain_two_grad[:, None]], axis=1)
-    columns = jnp.pad(columns, ((0, 0), (0, -columns.shape[1] % 128)))
-    row = jnp.pad(jnp.concatenate([q_gain_grad, k_gain_grad]), ((0, 6), (0, columns.shape[1] - HEAD_SIZE)))
-    small = sum_small(columns, row, *head_parts)
+    lines = jnp.concatenate([router_grad, gain_one_grad, gain_two_grad[None]], axis=0)
+    small = sum_small(lines, jnp.concatenate([q_gain_grad, k_gain_grad], axis=1))
     for k in groups[1]:
         moe.append(home_sum(k, after(peer_gates, *head_parts)))
     moe = sum(moe[1:], moe[0])
@@ -948,19 +949,19 @@
     d_tokens, _ = row_norm_back(d_normed_one, wide_in, rinv_one, gain_one)
     token_grad = d_mid + d_tokens
 
-    rows_own = MODEL_WIDTH // ne
+    head_gains = small[experts + 2 :].reshape(-1)
     return (
         output,
         token_grad,
-        small[:rows_own, experts],
+        small[experts],
         share_heads[:, :width_q],
         share_heads[:, width_q : width_q + width_k],
         share_heads[:, width_q + width_k :],
         share_out,
-        small[rows_own, :HEAD_SIZE],
-        small[rows_own + 1, :HEAD_SIZE],
-        small[:rows_own, experts + 1],
-        small[:rows_own, :experts],
+        head_gains[:HEAD_SIZE],
+        head_gains[HEAD_SIZE : 2 * HEAD_SIZE],
+        small[experts + 1],
+        jnp.transpose(small[:experts]),
         gate_grad[None],
         up_grad[None],
         down_grad[None],

time: 1220 us -> 1190 us (0.975)
  the two profiles are of different devices: /device:TPU:21 before, /device:TPU:0 now
where the time goes in v1:
time: 1190 us; the launch traced here: 1180 us
  Pallas kernels  544 us (46%)
  starting transfers between devices  226 us (19%)
  waiting for transfers between devices  216 us (18%)
  other arithmetic  68 us (6%)
  local copies, waits for them, and re-layouts  62.7 us (5%)
  matrix products  55.8 us (5%)
    pallas_call x1, Pallas kernels, run_experts(): pl.pallas_call(lambda *refs: experts_kernel(nf, nz, cap, *refs), in_specs...  386 us
    ppermute x21, starting transfers between devices, along(): lax.ppermute(value, 'expert', [(j, (j + 2 * k) % ne) for j in range(ne)])  168 us
    ppermute x51, waiting for transfers between devices, across(): lax.ppermute(value, ALL, [(i * ne + j, (i ^ df) * ne + (j ^ dc)) for i in...  116 us
    ppermute x21, waiting for transfers between devices, along(): lax.ppermute(value, 'expert', [(j, (j + 2 * k) % ne) for j in range(ne)])  98 us
    pallas_call x4, Pallas kernels, attend_back(): pl.pallas_call(lambda *refs: attend_back_kernel(len(w_blocks), heads, kv_...  56.3 us
    dot_general x6, matrix products, left_product(): lax.dot_general(left, right, (((0,), (0,)), ((), ())), preferred_element_...  51.7 us
    pallas_call x4, Pallas kernels, attend(): pl.pallas_call(lambda *refs: attend_kernel(len(w_blocks), heads, kv_heads...  43.5 us
    ppermute x51, starting transfers between devices, across(): lax.ppermute(value, ALL, [(i * ne + j, (i ^ df) * ne + (j ^ dc)) for i in...  39.6 us
  transfers between devices with their start and end apart: 75, of which 23 were waited for; matrix products, arithmetic and copies ran while one was open for 12% of the time, Pallas kernels for 13%

profile of v1, /device:TPU:0, one launch (start us, length us, event | category | flops | bytes accessed | tf_op | source)
XLA Modules:
  0.0 1176.1 jit_solution(13124720003840878097)
XLA Ops:
  4.1 5.1 collective-permute-start.3
  33.1 12.9 %collective-permute-done.9.refs_13_.refs_26_ = bf16[256,1280]{1,0:T(8,128)(2,1)S(1)} collective-permute-done((bf16[256,1280]{1,0:T(8,128)(2,1)S(1)}, bf16[256,1280]{1,0:T(8,128)(2,1)S(1)}, u32[]{:S(2)}, u32[]{:S(2)}) %collective-permute-start.9) | collective-permute-done | bytes 655392 | tf_op jit(solution)/shard_map/ppermute | solution.py:706
  79.6 13.4 %collective-permute-start.22 = (bf16[128,2048]{1,0:T(8,128)(2,1)}, bf16[128,2048]{1,0:T(8,128)(2,1)}, u32[]{:S(2)}, u32[]{:S(2)}) collective-permute-start(bf16[128,2048]{1,0:T(8,128)(2,1)} %refs_14_.3), channel_id=1, source_target_pairs={{0,6},{1,7},{2,0},{3,1},{4,2},{5,3},{6,4},{7,5},{8,14},{9,15},{10,... | collective-permute-start | bytes 1572872 | tf_op jit(solution)/shard_map/ppermute | solution.py:706
  92.9 5.8 collective-permute-start.18
  99.4 10.9 attend.4
  110.2 9.4 collective-permute-done.14.refs_1_.refs_2_
  119.6 10.8 attend.5
  130.4 11.0 attend.6
  146.5 5.9 project.4
  153.9 5.9 project.5
  160.3 5.9 project.6
  167.7 3.9 gather_slots.1
  177.7 10.8 attend.7
  188.5 6.2 project.7
  194.7 13.9 %collective-permute-done.28.refs_10_ = bf16[80,2176]{1,0:T(8,128)(2,1)S(1)} collective-permute-done((bf16[80,2176]{1,0:T(8,128)(2,1)}, bf16[80,2176]{1,0:T(8,128)(2,1)S(1)}, u32[]{:S(2)}, u32[]{:S(2)}) %collective-permute-start.28) | collective-permute-done | bytes 348192 | tf_op jit(solution)/shard_map/ppermute | solution.py:701
  209.5 5.0 collective-permute-done.29.refs_11_
  215.9 10.5 collective-permute-start.34
  236.8 8.5 collective-permute-done.32.refs_14_
  245.3 4.3 collective-permute-done.33.refs_15_
  249.6 5.2 collective-permute-done.34.refs_16_
  254.8 46.7 %collective-permute-done.35.refs_17_ = bf16[256,2176]{1,0:T(8,128)(2,1)S(1)} collective-permute-done((bf16[256,2176]{1,0:T(8,128)(2,1)S(1)}, bf16[256,2176]{1,0:T(8,128)(2,1)S(1)}, u32[]{:S(2)}, u32[]{:S(2)}) %collective-permute-start.35) | collective-permute-done | bytes 1114144 | tf_op jit(solution)/shard_map/ppermute | solution.py:706
  302.9 386.5 %run_experts.1 = (f32[256,2176]{1,0:T(8,128)}, bf16[4,640,2048]{2,1,0:T(8,128)(2,1)}, bf16[4,256,2048]{2,1,0:T(8,128)(2,1)}, bf16[4,640,2048]{2,1,0:T(8,128)(2,1...) custom-call(s32[1]{0:T(128)} %bitcast.44.refs_0_, ...), custom_call_target="tpu_custom_call" | custom-call | flops 48318382080 | bytes 600000000 | tf_op jit(solution)/shard_map/run_experts/pallas_call | solution.py:421
  703.8 12.7 %convolution_bitcast_fusion.1 = f32[1,2048,768]{2,1,0:T(8,128)} fusion(bf16[2560,2048]{1,0:T(8,128)(2,1)S(1)} %bitcast.285, bf16[2560,768]{1,0:T(8,128)(2,1)} %bitcast.289), kind=kOutput, calls=%fused_computation.24 | convolution fusion | flops 8053063680 | bytes 20709376 | tf_op jit(solution)/shard_map/dot_general | solution.py:39
  716.6 11.4 convolution_bitcast_fusion.2
  730.1 10.7 convolution_bitcast_fusion
  747.5 14.3 %attend_back.4 = (bf16[256,1280]{1,0:T(8,128)(2,1)}, f32[256,2048]{1,0:T(8,128)}, f32[1,2048]{1,0:T(1,128)}, f32[1,128]{1,0:T(1,128)}, f32[1,128]{1,0:T(1,128)}) custom-call(s32[8]{0:T(128)} %stack.107.refs_0_, bf16[256,2048]{1,0:T(8,128)(2,1)} %copy-done.26, bf16[256,2048]{1,0:T(8,128)(2,1)} %refs_2_.5, s32[1,256]{1,0:T(1,128)} %refs_3_.3, ...), custom_call_target="tpu_custom_call" | custom-call | flops 3355443200 | bytes 23068672 | tf_op jit(solution)/shard_map/attend_back/pallas_call | solution.py:657
  761.9 4.6 slice_bitcast_fusion.1
  769.6 6.8 fusion
  794.0 13.9 %attend_back.5 = (bf16[256,1280]{1,0:T(8,128)(2,1)}, bf16[256,2048]{1,0:T(8,128)(2,1)}, f32[1,2048]{1,0:T(1,128)}, f32[1,128]{1,0:T(1,128)}, f32[1,128]{1,0:T(1,128)}) custom-call(s32[8]{0:T(128)} %stack.107.refs_0_, bf16[256,2048]{1,0:T(8,128)(2,1)} %collective-permute-done.37.refs_1_, bf16[256,2048]{1,0:T(8,128)(2,1)} %collective-permute-done.refs_1_.refs_2_, ...), custom_call_target="tpu_custom_call" | custom-call | flops 3355443200 | bytes 23068672 | tf_op jit(solution)/shard_map/attend_back/pallas_call | solution.py:657
  811.9 14.1 %attend_back.6 = (bf16[256,1280]{1,0:T(8,128)(2,1)}, bf16[256,2048]{1,0:T(8,128)(2,1)}, f32[1,2048]{1,0:T(1,128)}, f32[1,128]{1,0:T(1,128)}, f32[1,128]{1,0:T(1,128)}) custom-call(s32[8]{0:T(128)} %stack.107.refs_0_, bf16[256,2048]{1,0:T(8,128)(2,1)} %collective-permute-done.38.refs_1_, bf16[256,2048]{1,0:T(8,128)(2,1)} %collective-permute-done.14.refs_1_.refs_2_, ...), custom_call_target="tpu_custom_call" | custom-call | flops 3355443200 | bytes 23068672 | tf_op jit(solution)/shard_map/attend_back/pallas_call | solution.py:657
  827.9 3.4 bitcast_add_fusion.1
  840.2 39.8 %collective-permute-start.73 = (bf16[128,2048]{1,0:T(8,128)(2,1)}, bf16[128,2048]{1,0:T(8,128)(2,1)}, u32[]{:S(2)}, u32[]{:S(2)}) collective-permute-start(bf16[128,2048]{1,0:T(8,128)(2,1)} %get-tuple-element.244), channel_id=1, source_target_pairs={{0,4},{1,5},{2,6},{3,7},{4,0},{5,1},{6,2},{7,3},{8,12},{9,13},{10,... | collective-permute-start | bytes 1572872 | tf_op jit(solution)/shard_map/ppermute | solution.py:706
  880.1 7.6 combine_slots.5
  887.6 7.5 combine_slots.4
  895.3 14.0 %attend_back.7 = (bf16[256,1280]{1,0:T(8,128)(2,1)}, bf16[256,2048]{1,0:T(8,128)(2,1)}, f32[1,2048]{1,0:T(1,128)}, f32[1,128]{1,0:T(1,128)}, f32[1,128]{1,0:T(1,128)}) custom-call(s32[8]{0:T(128)} %stack.107.refs_0_, bf16[256,2048]{1,0:T(8,128)(2,1)} %collective-permute-done.39.refs_1_, bf16[256,2048]{1,0:T(8,128)(2,1)} %collective-permute-done.13.refs_1_.refs_2_, ...), custom_call_target="tpu_custom_call" | custom-call | flops 3355443200 | bytes 23068672 | tf_op jit(solution)/shard_map/attend_back/pallas_call | solution.py:657
  911.6 9.1 fusion.8
  920.9 17.3 %collective-permute-start.64 = (f32[40,256]{1,0:T(8,128)S(1)}, f32[40,256]{1,0:T(8,128)S(1)}, u32[]{:S(2)}, u32[]{:S(2)}) collective-permute-start(f32[40,256]{1,0:T(8,128)S(1)} %get-tuple-element.249), channel_id=1, source_target_pairs={{0,4},{1,5},{2,6},{3,7},{4,0},{5,1},{6,2},{7,3},{8,12},{9,13},{10,... | collective-permute-start | bytes 122888 | tf_op jit(solution)/shard_map/ppermute | solution.py:758
  949.3 7.9 collective-permute-done.74
  959.8 6.1 collective-permute-done.60
  967.1 23.7 %collective-permute-done.61 = bf16[256,2048]{1,0:T(8,128)(2,1)S(1)} collective-permute-done((bf16[256,2048]{1,0:T(8,128)(2,1)S(1)}, bf16[256,2048]{1,0:T(8,128)(2,1)S(1)}, u32[]{:S(2)}, u32[]{:S(2)}) %collective-permute-start.61) | collective-permute-done | bytes 1048608 | tf_op jit(solution)/shard_map/ppermute | solution.py:701
  995.1 7.2 collective-permute-done.57.refs_7_
  1004.7 14.2 %collective-permute-done.56.refs_6_ = bf16[160,2048]{1,0:T(8,128)(2,1)S(1)} collective-permute-done((bf16[160,2048]{1,0:T(8,128)(2,1)S(1)}, bf16[160,2048]{1,0:T(8,128)(2,1)S(1)}, u32[]{:S(2)}, u32[]{:S(2)}) %collective-permute-start.56) | collective-permute-done | bytes 655392 | tf_op jit(solution)/shard_map/ppermute | solution.py:701
  1024.7 7.0 collective-permute-done.55.refs_5_
  1033.4 12.3 %collective-permute-done.54.refs_4_ = bf16[160,2048]{1,0:T(8,128)(2,1)} collective-permute-done((bf16[160,2048]{1,0:T(8,128)(2,1)}, bf16[160,2048]{1,0:T(8,128)(2,1)}, u32[]{:S(2)}, u32[]{:S(2)}) %collective-permute-start.54) | collective-permute-done | bytes 655392 | tf_op jit(solution)/shard_map/ppermute | solution.py:701
  1046.2 7.7 combine_slots.7
  1057.4 7.5 combine_slots.6
  1073.6 71.5 %collective-permute-start.58 = (bf16[256,2048]{1,0:T(8,128)(2,1)}, bf16[256,2048]{1,0:T(8,128)(2,1)S(1)}, u32[]{:S(2)}, u32[]{:S(2)}) collective-permute-start(bf16[256,2048]{1,0:T(8,128)(2,1)} %combine_slots.6), channel_id=1, source_target_pairs={{0,2},{1,3},{2,4},{3,5},{4,6},{5,7},{6,0},{7,1},{8,10},{9,11},{10,... | collective-permute-start | bytes 3145736 | tf_op jit(solution)/shard_map/ppermute | solution.py:706
  1146.2 22.1 %collective-permute-done.70 = bf16[256,1280]{1,0:T(8,128)(2,1)} collective-permute-done((bf16[256,1280]{1,0:T(8,128)(2,1)}, bf16[256,1280]{1,0:T(8,128)(2,1)}, u32[]{:S(2)}, u32[]{:S(2)}) %collective-permute-start.70) | collective-permute-done | bytes 655392 | tf_op jit(solution)/shard_map/ppermute | solution.py:706
  (467 shorter events, 200.5 us)
Async XLA Ops:
  11.5 34.5 %collective-permute-start.9 = (bf16[256,1280]{1,0:T(8,128)(2,1)S(1)}, bf16[256,1280]{1,0:T(8,128)(2,1)S(1)}, u32[]{:S(2)}, u32[]{:S(2)}) collective-permute-start(bf16[256,1280]{1,0:T(8,128)(2,1)S(1)} %pad_maximum_fusion.1.refs_9_.refs_22_), channel_id=1, source_target_pairs={{0,4},{1,5},{2,6},{3,7},{4,0},{5,1},{6,2},{7,3},{8,12},{9,13},{10,... | collective-permute-start | bytes 1966088 | tf_op jit(solution)/shard_map/ppermute | solution.py:706
  13.4 58.7 %collective-permute-start.11 = (bf16[256,1280]{1,0:T(8,128)(2,1)S(1)}, bf16[256,1280]{1,0:T(8,128)(2,1)S(1)}, u32[]{:S(2)}, u32[]{:S(2)}) collective-permute-start(bf16[256,1280]{1,0:T(8,128)(2,1)S(1)} %pad_maximum_fusion.1.refs_9_.refs_22_), channel_id=1, source_target_pairs={{0,6},{1,7},{2,0},{3,1},{4,2},{5,3},{6,4},{7,5},{8,14},{9,15},{10,... | collective-permute-start | bytes 1966088 | tf_op jit(solution)/shard_map/ppermute | solution.py:706
  21.4 51.5 %collective-permute-start.7 = (bf16[256,1280]{1,0:T(8,128)(2,1)S(1)}, bf16[256,1280]{1,0:T(8,128)(2,1)S(1)}, u32[]{:S(2)}, u32[]{:S(2)}) collective-permute-start(bf16[256,1280]{1,0:T(8,128)(2,1)S(1)} %pad_maximum_fusion.1.refs_9_.refs_22_), channel_id=1, source_target_pairs={{0,2},{1,3},{2,4},{3,5},{4,6},{5,7},{6,0},{7,1},{8,10},{9,11},{10,... | collective-permute-start | bytes 1966088 | tf_op jit(solution)/shard_map/ppermute | solution.py:706
  46.0 29.2 %collective-permute-start.6 = (bf16[256,1280]{1,0:T(8,128)(2,1)S(1)}, bf16[256,1280]{1,0:T(8,128)(2,1)S(1)}, u32[]{:S(2)}, u32[]{:S(2)}) collective-permute-start(bf16[256,1280]{1,0:T(8,128)(2,1)S(1)} %pad_maximum_fusion.1.refs_9_.refs_22_), channel_id=1, source_target_pairs={{0,1},{1,0},{2,3},{3,2},{4,5},{5,4},{6,7},{7,6},{8,9},{9,8},{10,11... | collective-permute-start | bytes 1966088 | tf_op jit(solution)/shard_map/ppermute | solution.py:701
  46.0 29.2 %collective-permute-start.10 = (bf16[256,1280]{1,0:T(8,128)(2,1)S(1)}, bf16[256,1280]{1,0:T(8,128)(2,1)}, u32[]{:S(2)}, u32[]{:S(2)}) collective-permute-start(bf16[256,1280]{1,0:T(8,128)(2,1)S(1)} %collective-permute-done.9.refs_13_.refs_26_), channel_id=1, source_target_pairs={{0,1},{1,0},{2,3},{3,2},{4,5},{5,4},{6,7},{7,6},{8,9},{9,8},{10,11... | collective-permute-start | bytes 1966088 | tf_op jit(solution)/shard_map/ppermute | solution.py:701
  61.4 31.6 %collective-permute-start = (bf16[256,2048]{1,0:T(8,128)(2,1)}, bf16[256,2048]{1,0:T(8,128)(2,1)}, u32[]{:S(2)}, u32[]{:S(2)}) collective-permute-start(bf16[256,2048]{1,0:T(8,128)(2,1)} %refs_2_.5), channel_id=1, source_target_pairs={{0,8},{1,9},{2,10},{3,11},{4,12},{5,13},{6,14},{7,15},{8,0},{9,1},... | collective-permute-start | bytes 3145736 | tf_op jit(solution)/shard_map/ppermute | solution.py:701
  72.2 47.4 %collective-permute-start.14 = (bf16[256,2048]{1,0:T(8,128)(2,1)}, bf16[256,2048]{1,0:T(8,128)(2,1)}, u32[]{:S(2)}, u32[]{:S(2)}) collective-permute-start(bf16[256,2048]{1,0:T(8,128)(2,1)} %refs_2_.5), channel_id=1, source_target_pairs={{0,16},{1,17},{2,18},{3,19},{4,20},{5,21},{6,22},{7,23},{8,24},{9,... | collective-permute-start | bytes 3145736 | tf_op jit(solution)/shard_map/ppermute | solution.py:701
  72.8 57.6 %collective-permute-start.13 = (bf16[256,2048]{1,0:T(8,128)(2,1)}, bf16[256,2048]{1,0:T(8,128)(2,1)}, u32[]{:S(2)}, u32[]{:S(2)}) collective-permute-start(bf16[256,2048]{1,0:T(8,128)(2,1)} %refs_2_.5), channel_id=1, source_target_pairs={{0,24},{1,25},{2,26},{3,27},{4,28},{5,29},{6,30},{7,31},{8,16},{9,... | collective-permute-start | bytes 3145736 | tf_op jit(solution)/shard_map/ppermute | solution.py:701
  79.6 62.0 %collective-permute-start.22 = (bf16[128,2048]{1,0:T(8,128)(2,1)}, bf16[128,2048]{1,0:T(8,128)(2,1)}, u32[]{:S(2)}, u32[]{:S(2)}) collective-permute-start(bf16[128,2048]{1,0:T(8,128)(2,1)} %refs_14_.3), channel_id=1, source_target_pairs={{0,6},{1,7},{2,0},{3,1},{4,2},{5,3},{6,4},{7,5},{8,14},{9,15},{10,... | collective-permute-start | bytes 1572872 | tf_op jit(solution)/shard_map/ppermute | solution.py:706
  92.9 49.1 %collective-permute-start.20 = (bf16[128,2048]{1,0:T(8,128)(2,1)}, bf16[128,2048]{1,0:T(8,128)(2,1)}, u32[]{:S(2)}, u32[]{:S(2)}) collective-permute-start(bf16[128,2048]{1,0:T(8,128)(2,1)} %refs_14_.3), channel_id=1, source_target_pairs={{0,4},{1,5},{2,6},{3,7},{4,0},{5,1},{6,2},{7,3},{8,12},{9,13},{10,... | collective-permute-start | bytes 1572872 | tf_op jit(solution)/shard_map/ppermute | solution.py:706
  92.9 49.2 %collective-permute-start.18 = (bf16[128,2048]{1,0:T(8,128)(2,1)}, bf16[128,2048]{1,0:T(8,128)(2,1)}, u32[]{:S(2)}, u32[]{:S(2)}) collective-permute-start(bf16[128,2048]{1,0:T(8,128)(2,1)} %refs_14_.3), channel_id=1, source_target_pairs={{0,2},{1,3},{2,4},{3,5},{4,6},{5,7},{6,0},{7,1},{8,10},{9,11},{10,... | collective-permute-start | bytes 1572872 | tf_op jit(solution)/shard_map/ppermute | solution.py:706
  152.4 63.4 %collective-permute-start.24 = (bf16[256,2048]{1,0:T(8,128)(2,1)}, bf16[256,2048]{1,0:T(8,128)(2,1)}, u32[]{:S(2)}, u32[]{:S(2)}) collective-permute-start(bf16[256,2048]{1,0:T(8,128)(2,1)} %project.4), channel_id=1, source_target_pairs={{0,8},{1,9},{2,10},{3,11},{4,12},{5,13},{6,14},{7,15},{8,0},{9,1},... | collective-permute-start | bytes 3145736 | tf_op jit(solution)/shard_map/ppermute | solution.py:701
  159.8 66.6 %collective-permute-start.25 = (bf16[256,2048]{1,0:T(8,128)(2,1)}, bf16[256,2048]{1,0:T(8,128)(2,1)}, u32[]{:S(2)}, u32[]{:S(2)}) collective-permute-start(bf16[256,2048]{1,0:T(8,128)(2,1)} %project.5), channel_id=1, source_target_pairs={{0,16},{1,17},{2,18},{3,19},{4,20},{5,21},{6,22},{7,23},{8,24},{9,... | collective-permute-start | bytes 3145736 | tf_op jit(solution)/shard_map/ppermute | solution.py:701
  166.1 63.7 %collective-permute-start.26 = (bf16[256,2048]{1,0:T(8,128)(2,1)}, bf16[256,2048]{1,0:T(8,128)(2,1)}, u32[]{:S(2)}, u32[]{:S(2)}) collective-permute-start(bf16[256,2048]{1,0:T(8,128)(2,1)} %project.6), channel_id=1, source_target_pairs={{0,24},{1,25},{2,26},{3,27},{4,28},{5,29},{6,30},{7,31},{8,16},{9,... | collective-permute-start | bytes 3145736 | tf_op jit(solution)/shard_map/ppermute | solution.py:701
  174.3 34.4 %collective-permute-start.28 = (bf16[80,2176]{1,0:T(8,128)(2,1)}, bf16[80,2176]{1,0:T(8,128)(2,1)S(1)}, u32[]{:S(2)}, u32[]{:S(2)}) collective-permute-start(bf16[80,2176]{1,0:T(8,128)(2,1)} %get-tuple-element.123), channel_id=1, source_target_pairs={{0,8},{1,9},{2,10},{3,11},{4,12},{5,13},{6,14},{7,15},{8,0},{9,1},... | collective-permute-start | bytes 1044488 | tf_op jit(solution)/shard_map/ppermute | solution.py:701
  175.8 38.7 %collective-permute-start.29 = (bf16[80,2176]{1,0:T(8,128)(2,1)}, bf16[80,2176]{1,0:T(8,128)(2,1)}, u32[]{:S(2)}, u32[]{:S(2)}) collective-permute-start(bf16[80,2176]{1,0:T(8,128)(2,1)} %get-tuple-element.124), channel_id=1, source_target_pairs={{0,9},{1,8},{2,11},{3,10},{4,13},{5,12},{6,15},{7,14},{8,1},{9,0},... | collective-permute-start | bytes 1044488 | tf_op jit(solution)/shard_map/ppermute | solution.py:701
  215.9 38.9 %collective-permute-start.34 = (bf16[256,2176]{1,0:T(8,128)(2,1)S(1)}, bf16[256,2176]{1,0:T(8,128)(2,1)S(1)}, u32[]{:S(2)}, u32[]{:S(2)}) collective-permute-start(bf16[256,2176]{1,0:T(8,128)(2,1)S(1)} %copy-done.44), channel_id=1, source_target_pairs={{0,2},{1,3},{2,4},{3,5},{4,6},{5,7},{6,0},{7,1},{8,10},{9,11},{10,... | collective-permute-start | bytes 3342344 | tf_op jit(solution)/shard_map/ppermute | solution.py:706
  226.4 75.1 %collective-permute-start.35 = (bf16[256,2176]{1,0:T(8,128)(2,1)S(1)}, bf16[256,2176]{1,0:T(8,128)(2,1)S(1)}, u32[]{:S(2)}, u32[]{:S(2)}) collective-permute-start(bf16[256,2176]{1,0:T(8,128)(2,1)S(1)} %copy-done.44), channel_id=1, source_target_pairs={{0,4},{1,5},{2,6},{3,7},{4,0},{5,1},{6,2},{7,3},{8,12},{9,13},{10,... | collective-permute-start | bytes 3342344 | tf_op jit(solution)/shard_map/ppermute | solution.py:706
  229.8 71.7 %collective-permute-start.36 = (bf16[256,2176]{1,0:T(8,128)(2,1)S(1)}, bf16[256,2176]{1,0:T(8,128)(2,1)S(1)}, u32[]{:S(2)}, u32[]{:S(2)}) collective-permute-start(bf16[256,2176]{1,0:T(8,128)(2,1)S(1)} %copy-done.44), channel_id=1, source_target_pairs={{0,6},{1,7},{2,0},{3,1},{4,2},{5,3},{6,4},{7,5},{8,14},{9,15},{10,... | collective-permute-start | bytes 3342344 | tf_op jit(solution)/shard_map/ppermute | solution.py:706
  699.4 62.5 %collective-permute-start.37 = (bf16[256,2048]{1,0:T(8,128)(2,1)S(1)}, bf16[256,2048]{1,0:T(8,128)(2,1)}, u32[]{:S(2)}, u32[]{:S(2)}) collective-permute-start(bf16[256,2048]{1,0:T(8,128)(2,1)S(1)} %get-tuple-element.202.refs_1_), channel_id=1, source_target_pairs={{0,8},{1,9},{2,10},{3,11},{4,12},{5,13},{6,14},{7,15},{8,0},{9,1},... | collective-permute-start | bytes 3145736 | tf_op jit(solution)/shard_map/ppermute | solution.py:701
  700.8 61.1 %collective-permute-start.38 = (bf16[256,2048]{1,0:T(8,128)(2,1)S(1)}, bf16[256,2048]{1,0:T(8,128)(2,1)}, u32[]{:S(2)}, u32[]{:S(2)}) collective-permute-start(bf16[256,2048]{1,0:T(8,128)(2,1)S(1)} %get-tuple-element.202.refs_1_), channel_id=1, source_target_pairs={{0,16},{1,17},{2,18},{3,19},{4,20},{5,21},{6,22},{7,23},{8,24},{9,... | collective-permute-start | bytes 3145736 | tf_op jit(solution)/shard_map/ppermute | solution.py:701
  702.0 59.8 %collective-permute-start.39 = (bf16[256,2048]{1,0:T(8,128)(2,1)S(1)}, bf16[256,2048]{1,0:T(8,128)(2,1)}, u32[]{:S(2)}, u32[]{:S(2)}) collective-permute-start(bf16[256,2048]{1,0:T(8,128)(2,1)S(1)} %get-tuple-element.202.refs_1_), channel_id=1, source_target_pairs={{0,24},{1,25},{2,26},{3,27},{4,28},{5,29},{6,30},{7,31},{8,16},{9,... | collective-permute-start | bytes 3145736 | tf_op jit(solution)/shard_map/ppermute | solution.py:701
  778.4 49.3 %collective-permute-start.40 = (bf16[4,128,2048]{2,1,0:T(8,128)(2,1)}, bf16[4,128,2048]{2,1,0:T(8,128)(2,1)}, u32[]{:S(2)}, u32[]{:S(2)}) collective-permute-start(bf16[4,128,2048]{2,1,0:T(8,128)(2,1)} %fusion.34), channel_id=1, source_target_pairs={{0,1},{1,0},{2,3},{3,2},{4,5},{5,4},{6,7},{7,6},{8,9},{9,8},{10,11... | collective-permute-start | bytes 6291464 | tf_op jit(solution)/shard_map/ppermute | solution.py:701
  779.8 46.1 %collective-permute-start.47 = (bf16[160,2048]{1,0:T(8,128)(2,1)}, bf16[160,2048]{1,0:T(8,128)(2,1)S(1)}, u32[]{:S(2)}, u32[]{:S(2)}) collective-permute-start(bf16[160,2048]{1,0:T(8,128)(2,1)} %pad_maximum_fusion.9), channel_id=1, source_target_pairs={{0,25},{1,24},{2,27},{3,26},{4,29},{5,28},{6,31},{7,30},{8,17},{9,... | collective-permute-start | bytes 1966088 | tf_op jit(solution)/shard_map/ppermute | solution.py:701
  782.5 44.6 %collective-permute-start.46 = (bf16[160,2048]{1,0:T(8,128)(2,1)}, bf16[160,2048]{1,0:T(8,128)(2,1)S(1)}, u32[]{:S(2)}, u32[]{:S(2)}) collective-permute-start(bf16[160,2048]{1,0:T(8,128)(2,1)} %pad_maximum_fusion.8), channel_id=1, source_target_pairs={{0,24},{1,25},{2,26},{3,27},{4,28},{5,29},{6,30},{7,31},{8,16},{9,... | collective-permute-start | bytes 1966088 | tf_op jit(solution)/shard_map/ppermute | solution.py:701
  784.1 51.6 %collective-permute-start.45 = (bf16[160,2048]{1,0:T(8,128)(2,1)}, bf16[160,2048]{1,0:T(8,128)(2,1)}, u32[]{:S(2)}, u32[]{:S(2)}) collective-permute-start(bf16[160,2048]{1,0:T(8,128)(2,1)} %pad_maximum_fusion.7), channel_id=1, source_target_pairs={{0,17},{1,16},{2,19},{3,18},{4,21},{5,20},{6,23},{7,22},{8,25},{9,... | collective-permute-start | bytes 1966088 | tf_op jit(solution)/shard_map/ppermute | solution.py:701
  786.1 54.1 %collective-permute-start.44 = (bf16[160,2048]{1,0:T(8,128)(2,1)}, bf16[160,2048]{1,0:T(8,128)(2,1)}, u32[]{:S(2)}, u32[]{:S(2)}) collective-permute-start(bf16[160,2048]{1,0:T(8,128)(2,1)} %pad_maximum_fusion.6), channel_id=1, source_target_pairs={{0,16},{1,17},{2,18},{3,19},{4,20},{5,21},{6,22},{7,23},{8,24},{9,... | collective-permute-start | bytes 1966088 | tf_op jit(solution)/shard_map/ppermute | solution.py:701
  826.0 54.1 %collective-permute-start.43 = (bf16[160,2048]{1,0:T(8,128)(2,1)}, bf16[160,2048]{1,0:T(8,128)(2,1)}, u32[]{:S(2)}, u32[]{:S(2)}) collective-permute-start(bf16[160,2048]{1,0:T(8,128)(2,1)} %pad_maximum_fusion.5), channel_id=1, source_target_pairs={{0,9},{1,8},{2,11},{3,10},{4,13},{5,12},{6,15},{7,14},{8,1},{9,0},... | collective-permute-start | bytes 1966088 | tf_op jit(solution)/shard_map/ppermute | solution.py:701
  827.1 53.0 %collective-permute-start.42 = (bf16[160,2048]{1,0:T(8,128)(2,1)}, bf16[160,2048]{1,0:T(8,128)(2,1)}, u32[]{:S(2)}, u32[]{:S(2)}) collective-permute-start(bf16[160,2048]{1,0:T(8,128)(2,1)} %pad_maximum_fusion.4), channel_id=1, source_target_pairs={{0,8},{1,9},{2,10},{3,11},{4,12},{5,13},{6,14},{7,15},{8,0},{9,1},... | collective-permute-start | bytes 1966088 | tf_op jit(solution)/shard_map/ppermute | solution.py:701
  827.6 52.5 %collective-permute-start.41 = (bf16[160,2048]{1,0:T(8,128)(2,1)}, bf16[160,2048]{1,0:T(8,128)(2,1)}, u32[]{:S(2)}, u32[]{:S(2)}) collective-permute-start(bf16[160,2048]{1,0:T(8,128)(2,1)} %pad_maximum_fusion.3), channel_id=1, source_target_pairs={{0,1},{1,0},{2,3},{3,2},{4,5},{5,4},{6,7},{7,6},{8,9},{9,8},{10,11... | collective-permute-start | bytes 1966088 | tf_op jit(solution)/shard_map/ppermute | solution.py:701
  835.7 110.5 %collective-permute-start.72 = (bf16[128,2048]{1,0:T(8,128)(2,1)}, bf16[128,2048]{1,0:T(8,128)(2,1)S(1)}, u32[]{:S(2)}, u32[]{:S(2)}) collective-permute-start(bf16[128,2048]{1,0:T(8,128)(2,1)} %get-tuple-element.245), channel_id=1, source_target_pairs={{0,2},{1,3},{2,4},{3,5},{4,6},{5,7},{6,0},{7,1},{8,10},{9,11},{10,... | collective-permute-start | bytes 1572872 | tf_op jit(solution)/shard_map/ppermute | solution.py:706
  840.2 105.9 %collective-permute-start.73 = (bf16[128,2048]{1,0:T(8,128)(2,1)}, bf16[128,2048]{1,0:T(8,128)(2,1)}, u32[]{:S(2)}, u32[]{:S(2)}) collective-permute-start(bf16[128,2048]{1,0:T(8,128)(2,1)} %get-tuple-element.244), channel_id=1, source_target_pairs={{0,4},{1,5},{2,6},{3,7},{4,0},{5,1},{6,2},{7,3},{8,12},{9,13},{10,... | collective-permute-start | bytes 1572872 | tf_op jit(solution)/shard_map/ppermute | solution.py:706
  941.1 26.0 %collective-permute-start.59 = (bf16[256,2048]{1,0:T(8,128)(2,1)S(1)}, bf16[256,2048]{1,0:T(8,128)(2,1)S(1)}, u32[]{:S(2)}, u32[]{:S(2)}) collective-permute-start(bf16[256,2048]{1,0:T(8,128)(2,1)S(1)} %copy-done.76), channel_id=1, source_target_pairs={{0,8},{1,9},{2,10},{3,11},{4,12},{5,13},{6,14},{7,15},{8,0},{9,1},... | collective-permute-start | bytes 3145736 | tf_op jit(solution)/shard_map/ppermute | solution.py:701
  946.1 73.1 %collective-permute-start.50 = (bf16[4,256,1280]{2,1,0:T(8,128)(2,1)S(1)}, bf16[4,256,1280]{2,1,0:T(8,128)(2,1)S(1)}, u32[]{:S(2)}, u32[]{:S(2)}) collective-permute-start(bf16[4,256,1280]{2,1,0:T(8,128)(2,1)S(1)} %fusion.17), channel_id=1, source_target_pairs={{0,1},{1,0},{2,3},{3,2},{4,5},{5,4},{6,7},{7,6},{8,9},{9,8},{10,11... | collective-permute-start | bytes 7864328 | tf_op jit(solution)/shard_map/ppermute | solution.py:701
  946.2 44.7 %collective-permute-start.61 = (bf16[256,2048]{1,0:T(8,128)(2,1)S(1)}, bf16[256,2048]{1,0:T(8,128)(2,1)S(1)}, u32[]{:S(2)}, u32[]{:S(2)}) collective-permute-start(bf16[256,2048]{1,0:T(8,128)(2,1)S(1)} %copy-done.78), channel_id=1, source_target_pairs={{0,24},{1,25},{2,26},{3,27},{4,28},{5,29},{6,30},{7,31},{8,16},{9,... | collective-permute-start | bytes 3145736 | tf_op jit(solution)/shard_map/ppermute | solution.py:701
  957.2 45.1 %collective-permute-start.57 = (bf16[160,2048]{1,0:T(8,128)(2,1)S(1)}, bf16[160,2048]{1,0:T(8,128)(2,1)S(1)}, u32[]{:S(2)}, u32[]{:S(2)}) collective-permute-start(bf16[160,2048]{1,0:T(8,128)(2,1)S(1)} %copy-done.48), channel_id=1, source_target_pairs={{0,25},{1,24},{2,27},{3,26},{4,29},{5,28},{6,31},{7,30},{8,17},{9,... | collective-permute-start | bytes 1966088 | tf_op jit(solution)/shard_map/ppermute | solution.py:701
  965.9 53.0 %collective-permute-start.56 = (bf16[160,2048]{1,0:T(8,128)(2,1)S(1)}, bf16[160,2048]{1,0:T(8,128)(2,1)S(1)}, u32[]{:S(2)}, u32[]{:S(2)}) collective-permute-start(bf16[160,2048]{1,0:T(8,128)(2,1)S(1)} %copy-done.47), channel_id=1, source_target_pairs={{0,24},{1,25},{2,26},{3,27},{4,28},{5,29},{6,30},{7,31},{8,16},{9,... | collective-permute-start | bytes 1966088 | tf_op jit(solution)/shard_map/ppermute | solution.py:701
  967.1 64.5 %collective-permute-start.55 = (bf16[160,2048]{1,0:T(8,128)(2,1)}, bf16[160,2048]{1,0:T(8,128)(2,1)}, u32[]{:S(2)}, u32[]{:S(2)}) collective-permute-start(bf16[160,2048]{1,0:T(8,128)(2,1)} %pad_maximum_fusion.15), channel_id=1, source_target_pairs={{0,17},{1,16},{2,19},{3,18},{4,21},{5,20},{6,23},{7,22},{8,25},{9,... | collective-permute-start | bytes 1966088 | tf_op jit(solution)/shard_map/ppermute | solution.py:701
  990.9 54.9 %collective-permute-start.54 = (bf16[160,2048]{1,0:T(8,128)(2,1)}, bf16[160,2048]{1,0:T(8,128)(2,1)}, u32[]{:S(2)}, u32[]{:S(2)}) collective-permute-start(bf16[160,2048]{1,0:T(8,128)(2,1)} %pad_maximum_fusion.14), channel_id=1, source_target_pairs={{0,16},{1,17},{2,18},{3,19},{4,20},{5,21},{6,22},{7,23},{8,24},{9,... | collective-permute-start | bytes 1966088 | tf_op jit(solution)/shard_map/ppermute | solution.py:701
  1002.2 43.9 %collective-permute-start.53 = (bf16[160,2048]{1,0:T(8,128)(2,1)}, bf16[160,2048]{1,0:T(8,128)(2,1)}, u32[]{:S(2)}, u32[]{:S(2)}) collective-permute-start(bf16[160,2048]{1,0:T(8,128)(2,1)} %pad_maximum_fusion.13), channel_id=1, source_target_pairs={{0,9},{1,8},{2,11},{3,10},{4,13},{5,12},{6,15},{7,14},{8,1},{9,0},... | collective-permute-start | bytes 1966088 | tf_op jit(solution)/shard_map/ppermute | solution.py:701
  1018.9 27.3 %collective-permute-start.52 = (bf16[160,2048]{1,0:T(8,128)(2,1)}, bf16[160,2048]{1,0:T(8,128)(2,1)}, u32[]{:S(2)}, u32[]{:S(2)}) collective-permute-start(bf16[160,2048]{1,0:T(8,128)(2,1)} %pad_maximum_fusion.12), channel_id=1, source_target_pairs={{0,8},{1,9},{2,10},{3,11},{4,12},{5,13},{6,14},{7,15},{8,0},{9,1},... | collective-permute-start | bytes 1966088 | tf_op jit(solution)/shard_map/ppermute | solution.py:701
  1019.3 26.9 %collective-permute-start.51 = (bf16[160,2048]{1,0:T(8,128)(2,1)}, bf16[160,2048]{1,0:T(8,128)(2,1)}, u32[]{:S(2)}, u32[]{:S(2)}) collective-permute-start(bf16[160,2048]{1,0:T(8,128)(2,1)} %pad_maximum_fusion.11), channel_id=1, source_target_pairs={{0,1},{1,0},{2,3},{3,2},{4,5},{5,4},{6,7},{7,6},{8,9},{9,8},{10,11... | collective-permute-start | bytes 1966088 | tf_op jit(solution)/shard_map/ppermute | solution.py:701
  1031.7 140.7 %collective-permute-start.49 = (bf16[256,2048]{1,0:T(8,128)(2,1)}, bf16[256,2048]{1,0:T(8,128)(2,1)}, u32[]{:S(2)}, u32[]{:S(2)}) collective-permute-start(bf16[256,2048]{1,0:T(8,128)(2,1)} %combine_slots.5), channel_id=1, source_target_pairs={{0,4},{1,5},{2,6},{3,7},{4,0},{5,1},{6,2},{7,3},{8,12},{9,13},{10,... | collective-permute-start | bytes 3145736 | tf_op jit(solution)/shard_map/ppermute | solution.py:706
  1045.7 27.9 %collective-permute-start.69 = (bf16[256,1280]{1,0:T(8,128)(2,1)}, bf16[256,1280]{1,0:T(8,128)(2,1)}, u32[]{:S(2)}, u32[]{:S(2)}) collective-permute-start(bf16[256,1280]{1,0:T(8,128)(2,1)} %get-tuple-element.242), channel_id=1, source_target_pairs={{0,2},{1,3},{2,4},{3,5},{4,6},{5,7},{6,0},{7,1},{8,10},{9,11},{10,... | collective-permute-start | bytes 1966088 | tf_op jit(solution)/shard_map/ppermute | solution.py:706
  1065.0 107.4 %collective-permute-start.48 = (bf16[256,2048]{1,0:T(8,128)(2,1)S(1)}, bf16[256,2048]{1,0:T(8,128)(2,1)}, u32[]{:S(2)}, u32[]{:S(2)}) collective-permute-start(bf16[256,2048]{1,0:T(8,128)(2,1)S(1)} %copy-done.45), channel_id=1, source_target_pairs={{0,6},{1,7},{2,0},{3,1},{4,2},{5,3},{6,4},{7,5},{8,14},{9,15},{10,... | collective-permute-start | bytes 3145736 | tf_op jit(solution)/shard_map/ppermute | solution.py:706
  1068.4 100.0 %collective-permute-start.70 = (bf16[256,1280]{1,0:T(8,128)(2,1)}, bf16[256,1280]{1,0:T(8,128)(2,1)}, u32[]{:S(2)}, u32[]{:S(2)}) collective-permute-start(bf16[256,1280]{1,0:T(8,128)(2,1)} %get-tuple-element.241), channel_id=1, source_target_pairs={{0,4},{1,5},{2,6},{3,7},{4,0},{5,1},{6,2},{7,3},{8,12},{9,13},{10,... | collective-permute-start | bytes 1966088 | tf_op jit(solution)/shard_map/ppermute | solution.py:706
  1068.4 99.9 %collective-permute-start.71 = (bf16[256,1280]{1,0:T(8,128)(2,1)}, bf16[256,1280]{1,0:T(8,128)(2,1)}, u32[]{:S(2)}, u32[]{:S(2)}) collective-permute-start(bf16[256,1280]{1,0:T(8,128)(2,1)} %get-tuple-element.240), channel_id=1, source_target_pairs={{0,6},{1,7},{2,0},{3,1},{4,2},{5,3},{6,4},{7,5},{8,14},{9,15},{10,... | collective-permute-start | bytes 1966088 | tf_op jit(solution)/shard_map/ppermute | solution.py:706
  1073.6 98.7 %collective-permute-start.58 = (bf16[256,2048]{1,0:T(8,128)(2,1)}, bf16[256,2048]{1,0:T(8,128)(2,1)S(1)}, u32[]{:S(2)}, u32[]{:S(2)}) collective-permute-start(bf16[256,2048]{1,0:T(8,128)(2,1)} %combine_slots.6), channel_id=1, source_target_pairs={{0,2},{1,3},{2,4},{3,5},{4,6},{5,7},{6,0},{7,1},{8,10},{9,11},{10,... | collective-permute-start | bytes 3145736 | tf_op jit(solution)/shard_map/ppermute | solution.py:706
  (120 other events, 2196.2 us)
